TPU v7x, 256 devices: a whole 4x4x8 slice. The times are simulated.
256 devices in a mesh: pair: 64 (over z, x_hi, y), occ: 4 (over x_lo, core).
Axes of the slice: x: 4 (x_hi: 2, x_lo: 2; x = x_hi * 2 + x_lo), y: 4, z: 8, core: 2. Of those that a mesh axis runs over, the one named last changes fastest.
Arguments:
- half_ints: bfloat16 [2, 896, 4, 896], P(None, 'pair', 'occ'), may hold values from -6 to 6
- coeffs: bfloat16 [896, 768], P('occ'), may hold values from -0.1875 to 0.1875
- pair_map: int32 [64], replicated, may hold values from 0 to 63, each once
- tile_table: int32 [64], replicated, may hold values from 0 to 63, each once
Outputs:
- mo_ints: float32 [1536, 4, 768], P('pair', 'occ')
Inputs may be any that keep to these rules, and one draw needn't show every extreme that they name: pair_map is a permutation of 0 to 63. tile_table is a permutation of 0 to 63.
All inputs are finite; a program needn't handle non-finite values.
Results may differ from a plain program's by a relative error of at most 0.0029.
Values may be sent and summed in bfloat16 or wider, within the bound.
No kernel may reach another device: no remote copies, remote signals or barrier semaphores. Data moves between devices by JAX's collectives and lax.ppermute only.
A program may use at most 64 MiB of HBM per device.

v0:
```python
import jax
import jax.numpy as jnp
from jax import lax
from jax.sharding import PartitionSpec as P


def joined_along(pieces, dim):
    shape = list(pieces.shape[1:])
    shape[dim] *= pieces.shape[0]
    return jnp.moveaxis(pieces, 0, dim).reshape(shape)


def sent_to_all(shard, axis):
    copies = jnp.broadcast_to(shard, (lax.axis_size(axis), *shard.shape))
    return lax.all_to_all(copies, axis, split_axis=0, concat_axis=0, tiled=True)


def gather_directly(shard, axis, dim):
    return joined_along(sent_to_all(shard, axis), dim)


def shards(half_ints, coeffs, pair_map, tile_table):
    num_occ = half_ints.shape[0]
    sblock = half_ints.shape[1]
    local_j = half_ints.shape[2]
    num_basis = half_ints.shape[3]
    num_virt = coeffs.shape[1]
    num_pair = lax.axis_size("pair")
    tile_rows = num_occ * num_virt // num_pair
    all_coeffs = gather_directly(coeffs, "occ", 0)
    flat_ints = half_ints.reshape(num_occ * sblock * local_j, num_basis)
    half_mo = jnp.dot(flat_ints, all_coeffs, preferred_element_type=jnp.float32).astype(
        jnp.bfloat16
    )
    half_mo = half_mo.reshape(num_occ, sblock, local_j, num_virt)
    tile_id = tile_table[lax.axis_index("pair")]
    virt_start = tile_id * tile_rows % num_virt
    column_coeffs = lax.dynamic_slice_in_dim(all_coeffs, virt_start, tile_rows, 1)
    half_flat = half_mo.reshape(num_occ, sblock, local_j * num_virt)
    slot_occ = tile_table * tile_rows // num_virt
    outgoing = jnp.take(half_flat, slot_occ, axis=0)
    incoming = lax.all_to_all(outgoing, "pair", split_axis=0, concat_axis=0, tiled=True)
    block_coeffs = jnp.take(column_coeffs.reshape(num_pair, sblock, tile_rows), pair_map, axis=0)
    result = jnp.einsum("psa,psc->ac", block_coeffs, incoming, preferred_element_type=jnp.float32)
    return result.reshape(tile_rows, local_j, num_virt)


def solution(mesh):
    placed = (P(None, "pair", "occ", None), P("occ", None), P(), P())
    return jax.shard_map(
        shards, mesh=mesh, in_specs=placed, out_specs=P("pair", "occ", None), check_vma=False
    )
```

profile of v0, /device:TPU:8, one launch (start us, length us, event | category | flops | bytes accessed | tf_op | source)
XLA Modules:
  0.0 81.8 jit_solution(3464739660900323313)
XLA Ops:
  0.0 2.2 %broadcast_in_dim.28 = bf16[4,224,768]{2,1,0:T(8,128)(2,1)} broadcast(bf16[224,768]{1,0:T(8,128)(2,1)} %param.5), dimensions={1,2} | broadcast | bytes 1720320 | tf_op jit(solution)/shard_map/broadcast_in_dim | solution.py:14
  2.2 0.0 copy-start
  2.2 0.0 copy-start.1
  2.2 3.7 %all-to-all-start = ((bf16[4,224,768]{2,1,0:T(8,128)(2,1)}), bf16[4,224,768]{2,1,0:T(8,128)(2,1)S(1)}, u32[]{:S(2)}, u32[]{:S(2)}) async-start(bf16[4,224,768]{2,1,0:T(8,128)(2,1)} %broadcast_in_dim.28), calls=%async_computation | async-start | bytes 2752512 | tf_op jit(solution)/shard_map/all_to_all | solution.py:15
  5.9 0.0 copy-done
  5.9 0.0 copy-done.1
  6.0 17.8 %all-to-all-done = bf16[4,224,768]{2,1,0:T(8,128)(2,1)S(1)} async-done(((bf16[4,224,768]{2,1,0:T(8,128)(2,1)}), bf16[4,224,768]{2,1,0:T(8,128)(2,1)S(1)}, u32[]{:S(2)}, u32[]{:S(2)}) %all-to-all-start) | async-done | bytes 1376288 | tf_op jit(solution)/shard_map/all_to_all | solution.py:15
  23.8 0.3 convolution_convert_fusion
  24.1 0.6 gather_fusion.1
  24.8 1.4 %broadcast_select_fusion = bf16[64,14,768]{2,1,0:T(8,128)(2,1)} fusion(bf16[64,14,768]{2,1,0:T(8,128)(2,1)S(1)} %gather_fusion.1, pred[64]{0:T(512)(128)(4,1)S(1)} %get-tuple-element.5), kind=kLoop, calls=%fused_computation.2 | loop fusion | flops 688128 | bytes 2752576 | tf_op jit(solution)/shard_map/jit(_take)/select_n | solution.py:41
  26.1 0.0 copy-start.2
  26.1 14.7 %all-to-all-start.1 = ((bf16[64,14,768]{2,1,0:T(8,128)(2,1)}), bf16[64,14,768]{2,1,0:T(8,128)(2,1)S(1)}, u32[]{:S(2)}, u32[]{:S(2)}) async-start(bf16[64,14,768]{2,1,0:T(8,128)(2,1)} %broadcast_select_fusion), calls=%async_computation.1 | async-start | bytes 3145728 | tf_op jit(solution)/shard_map/all_to_all | solution.py:42
  40.8 0.6 dynamic_slice.6
  42.1 0.0 copy-done.2
  42.1 0.1 constant_dynamic-slice_fusion
  42.3 0.1 reshape.49
  42.4 0.6 gather_fusion
  43.0 0.1 broadcast_select_fusion.1
  43.2 37.4 %all-to-all-done.1 = bf16[64,14,768]{2,1,0:T(8,128)(2,1)S(1)} async-done(((bf16[64,14,768]{2,1,0:T(8,128)(2,1)}), bf16[64,14,768]{2,1,0:T(8,128)(2,1)S(1)}, u32[]{:S(2)}, u32[]{:S(2)}) %all-to-all-start.1) | async-done | bytes 1376288 | tf_op jit(solution)/shard_map/all_to_all | solution.py:42
  80.6 0.5 fusion.2
  81.1 0.7 copy.23
  (8 shorter events, 0.1 us)
Async XLA Ops:
  2.2 3.7 %copy-start = (bf16[2,14,1,896]{3,0,2,1:T(2,128)(2,1)S(1)}, bf16[2,14,1,896]{3,0,2,1:T(2,128)(2,1)}, u32[]{:S(2)}) copy-start(bf16[2,14,1,896]{3,0,2,1:T(2,128)(2,1)} %param.4) | copy-start | bytes 150532
  2.2 3.7 %copy-start.1 = (s32[64]{0:T(128)S(1)}, s32[64]{0:T(128)}, u32[]{:S(2)}) copy-start(s32[64]{0:T(128)} %param.7) | copy-start | bytes 772
  2.2 21.6 %all-to-all-start = ((bf16[4,224,768]{2,1,0:T(8,128)(2,1)}), bf16[4,224,768]{2,1,0:T(8,128)(2,1)S(1)}, u32[]{:S(2)}, u32[]{:S(2)}) async-start(bf16[4,224,768]{2,1,0:T(8,128)(2,1)} %broadcast_in_dim.28), calls=%async_computation | async-start | bytes 2752512 | tf_op jit(solution)/shard_map/all_to_all | solution.py:15
  26.1 16.0 %copy-start.2 = (s32[64]{0:T(128)S(1)}, s32[64]{0:T(128)}, u32[]{:S(2)}) copy-start(s32[64]{0:T(128)} %param.6) | copy-start | bytes 772
  26.1 54.5 %all-to-all-start.1 = ((bf16[64,14,768]{2,1,0:T(8,128)(2,1)}), bf16[64,14,768]{2,1,0:T(8,128)(2,1)S(1)}, u32[]{:S(2)}, u32[]{:S(2)}) async-start(bf16[64,14,768]{2,1,0:T(8,128)(2,1)} %broadcast_select_fusion), calls=%async_computation.1 | async-start | bytes 3145728 | tf_op jit(solution)/shard_map/all_to_all | solution.py:42
where the time goes:
time: 82.2 us; the launch traced here: 81.8 us
  waiting for transfers between devices  55.3 us (67%)
  starting transfers between devices  18.4 us (22%)
  local copies, waits for them, and re-layouts  5.03 us (6%)
  other arithmetic  1.54 us (2%)
  matrix products  0.84 us (1%)
    all_to_all x1, waiting for transfers between devices, shards(): lax.all_to_all(outgoing, 'pair', split_axis=0, concat_axis=0, tiled=True)  37.4 us
    all_to_all x1, waiting for transfers between devices, sent_to_all(): return lax.all_to_all(copies, axis, split_axis=0, concat_axis=0, tiled=True)  17.8 us
    all_to_all x1, starting transfers between devices, shards(): lax.all_to_all(outgoing, 'pair', split_axis=0, concat_axis=0, tiled=True)  14.7 us
    all_to_all x1, starting transfers between devices, sent_to_all(): return lax.all_to_all(copies, axis, split_axis=0, concat_axis=0, tiled=True)  3.68 us
    broadcast_in_dim x1, local copies, waits for them, and re-layouts, sent_to_all(): copies = jnp.broadcast_to(shard, (lax.axis_size(axis), *shard.shape))  2.18 us
  transfers between devices with their start and end apart: 2, of which 2 were waited for; matrix products, arithmetic and copies ran while one was open for 2% of the time, Pallas kernels for 0%

commit v1 on v0

v1 whole, which is shorter than its diff:
```python
import jax
import jax.numpy as jnp
from jax import lax
from jax.sharding import Mesh, PartitionSpec as P

S1 = ("z",)
S2 = ("xh", "y")
OCC = ("xl", "c")


def swap(x, axis):
    return lax.ppermute(x, axis, [(0, 1), (1, 0)])


def shards(half_ints, coeffs, pair_map, tile_table):
    num_occ, sblock, _, nbf = half_ints.shape
    nvirt = coeffs.shape[1]
    rows = num_occ * nvirt // 64
    o = lax.axis_index(OCC)
    twin = swap(coeffs, "c")
    far = swap(coeffs, "xl")
    fartwin = swap(far, "c")
    nat = half_ints.reshape(num_occ * sblock, nbf)
    send = jnp.broadcast_to(nat, (8, *nat.shape))
    recv = lax.all_to_all(send, S1, 0, 0, tiled=True)
    full = jnp.zeros((4, *coeffs.shape), coeffs.dtype)
    for piece, k in ((coeffs, o), (twin, o ^ 1), (far, o ^ 2), (fartwin, o ^ 3)):
        full = lax.dynamic_update_index_in_dim(full, piece, k, 0)
    full = full.reshape(nbf, nvirt)
    half = jnp.dot(recv.reshape(-1, nbf), full, preferred_element_type=jnp.float32).astype(jnp.bfloat16)
    half = half.reshape(8, num_occ, sblock, nvirt)
    q = lax.axis_index(S2)
    z = lax.axis_index(S1)
    blocks = pair_map.reshape(8, 8)[:, q]
    tiles = tile_table.reshape(8, 8)[z]
    csel = jnp.take(full.reshape(64, sblock, nvirt), blocks, axis=0)
    cols = jnp.take(csel.reshape(8, sblock, nvirt // rows, rows), tiles % (nvirt // rows), axis=2)
    occ = tiles // (nvirt // rows)
    hot = (occ[:, None] == jnp.arange(num_occ)[None]).astype(jnp.bfloat16)
    left = jnp.einsum("stda,di->dasit", cols, hot).astype(jnp.bfloat16)
    part = jnp.einsum("dasit,sitb->dab", left, half, preferred_element_type=jnp.float32).astype(jnp.bfloat16)
    got = lax.all_to_all(part, S2, 0, 0, tiled=True)
    out = got.astype(jnp.float32).sum(0)
    return out.reshape(rows, 1, nvirt)


def solution(mesh):
    fine = Mesh(mesh.devices.reshape(8, 2, 4, 2, 2), ("z", "xh", "y", "xl", "c"))
    pair = ("z", "xh", "y")
    placed = (P(None, pair, OCC, None), P(OCC, None), P(), P())
    return jax.shard_map(shards, mesh=fine, in_specs=placed, out_specs=P(pair, OCC, None), check_vma=False)
```

time: 82.2 us -> 45.7 us (0.56)
  waiting for transfers between devices: 55.3 us -> 7.6 us
  blocking collectives: 0 us -> 14.9 us
  starting transfers between devices: 18.4 us -> 10.1 us
  local copies, waits for them, and re-layouts: 5.03 us -> 8.86 us
    all_to_all x2 -> x1, waiting for transfers between devices: 55.3 us -> 6.04 us  [shards(): recv = lax.all_to_all(send, S1, 0, 0, tiled=True)]
    all_to_all x0 -> x1, blocking collectives: none -> 14.9 us  [shards(): got = lax.all_to_all(part, S2, 0, 0, tiled=True)]
    all_to_all x2 -> x1, starting transfers between devices: 18.4 us -> 8.47 us  [shards(): recv = lax.all_to_all(send, S1, 0, 0, tiled=True)]
    gather x2 -> x3, local copies, waits for them, and re-layouts: 1.28 us -> 5.41 us  [the longest x2 3.59 us: shards(): csel = jnp.take(full.reshape(64, sblock, nvirt), blocks, axis=0)]
    ppermute x0 -> x3, starting transfers between devices: none -> 1.67 us  [swap(): return lax.ppermute(x, axis, [(0, 1), (1, 0)])]
    ppermute x0 -> x3, waiting for transfers between devices: none -> 1.56 us  [swap(): return lax.ppermute(x, axis, [(0, 1), (1, 0)])]
    broadcast_in_dim x1 -> x2, local copies, waits for them, and re-layouts: 2.18 us -> 0.9 us  [the longest x1 0.81 us: shards(): send = jnp.broadcast_to(nat, (8, *nat.shape))]
    select_n x3 -> x5, other arithmetic: 1.5 us -> 1.93 us  [the longest x2 1.71 us: shards(): csel = jnp.take(full.reshape(64, sblock, nvirt), blocks, axis=0)]
  transfers between devices with their start and end apart: 2 -> 4, of which waited for: 2 -> 2; matrix products, arithmetic and copies ran while one was open for 2% -> 23% of each run, Pallas kernels for 0% -> 0%
where the time goes in v1:
time: 45.7 us; the launch traced here: 44.9 us
  blocking collectives  14.9 us (33%)
  starting transfers between devices  10.1 us (22%)
  local copies, waits for them, and re-layouts  8.86 us (19%)
  waiting for transfers between devices  7.6 us (17%)
  other arithmetic  2.25 us (5%)
  matrix products  0.93 us (2%)
    all_to_all x1, blocking collectives, shards(): got = lax.all_to_all(part, S2, 0, 0, tiled=True)  14.9 us
    all_to_all x1, starting transfers between devices, shards(): recv = lax.all_to_all(send, S1, 0, 0, tiled=True)  8.47 us
    all_to_all x1, waiting for transfers between devices, shards(): recv = lax.all_to_all(send, S1, 0, 0, tiled=True)  6.04 us
    gather x2, local copies, waits for them, and re-layouts, shards(): csel = jnp.take(full.reshape(64, sblock, nvirt), blocks, axis=0)  3.59 us
    gather x1, local copies, waits for them, and re-layouts, shards(): jnp.take(csel.reshape(8, sblock, nvirt // rows, rows), tiles % (nvirt //...  1.82 us
    select_n x2, other arithmetic, shards(): csel = jnp.take(full.reshape(64, sblock, nvirt), blocks, axis=0)  1.71 us
    ppermute x3, starting transfers between devices, swap(): return lax.ppermute(x, axis, [(0, 1), (1, 0)])  1.67 us
    ppermute x3, waiting for transfers between devices, swap(): return lax.ppermute(x, axis, [(0, 1), (1, 0)])  1.56 us
  transfers between devices with their start and end apart: 4, of which 2 were waited for; matrix products, arithmetic and copies ran while one was open for 23% of the time, Pallas kernels for 0%

profile of v1, /device:TPU:8, one launch (start us, length us, event | category | flops | bytes accessed | tf_op | source)
XLA Modules:
  0.0 44.9 jit_solution(4172542460954863030)
XLA Ops:
  0.0 1.6 %collective-permute-start.1 = (bf16[224,768]{1,0:T(8,128)(2,1)}, bf16[224,768]{1,0:T(8,128)(2,1)S(1)}, u32[]{:S(2)}, u32[]{:S(2)}) collective-permute-start(bf16[224,768]{1,0:T(8,128)(2,1)} %param.5), channel_id=1, source_target_pairs={{0,2},{2,0},{1,3},{3,1},{4,6},{6,4},{5,7},{7,5},{8,10},{10,8},{9,1... | collective-permute-start | bytes 1032200 | tf_op jit(solution)/shard_map/ppermute | solution.py:12
  1.6 0.8 %copy.15 = bf16[2,14,1,896]{3,1,0,2:T(8,128)(2,1)S(1)} copy(bf16[2,14,1,896]{3,0,2,1:T(2,128)(2,1)} %param.4) | data formatting | bytes 100352 | tf_op args[0]
  2.4 0.8 %broadcast_in_dim.50 = bf16[8,28,896]{2,1,0:T(8,128)(2,1)} broadcast(bf16[28,896]{1,0:T(8,128)(2,1)S(1)} %reshape.125), dimensions={1,2} | broadcast | bytes 451584 | tf_op jit(solution)/shard_map/broadcast_in_dim | solution.py:24
  3.2 8.5 %all-to-all-start = ((bf16[8,28,896]{2,1,0:T(8,128)(2,1)}), bf16[8,28,896]{2,1,0:T(8,128)(2,1)S(1)}, u32[]{:S(2)}, u32[]{:S(2)}) async-start(bf16[8,28,896]{2,1,0:T(8,128)(2,1)} %broadcast_in_dim.50), calls=%async_computation | async-start | bytes 917504 | tf_op jit(solution)/shard_map/all_to_all | solution.py:25
  11.8 0.2 fusion.11
  12.0 0.2 and_reduce_fusion
  12.3 0.1 copy.11
  12.4 0.1 fusion.9
  12.6 0.1 broadcast_in_dim.43
  12.8 0.1 collective-permute-start.2
  12.9 1.6 %collective-permute-done.2 = bf16[224,768]{1,0:T(8,128)(2,1)S(1)} collective-permute-done((bf16[224,768]{1,0:T(8,128)(2,1)S(1)}, bf16[224,768]{1,0:T(8,128)(2,1)S(1)}, u32[]{:S(2)}, u32[]{:S(2)}) %collective-permute-start.2) | collective-permute-done | bytes 344096 | tf_op jit(solution)/shard_map/ppermute | solution.py:12
  14.5 0.4 reshape_reshape.3
  15.0 1.2 %gather_fusion = bf16[8,14,768]{2,1,0:T(8,128)(2,1)} fusion(bf16[64,14,768]{2,1,0:T(8,128)(2,1)S(1)} %reshape_reshape.3, s32[1024]{0:T(1024)S(1)} %pad_clamp_fusion.1), kind=kCustom, calls=%fused_computation | custom fusion | bytes 344096 | tf_op jit(solution)/shard_map/jit(_take)/gather | solution.py:36
  16.2 2.4 %reshape.147 = bf16[8,14,32,24]{3,2,1,0:T(8,128)(2,1)S(1)} reshape(bf16[8,14,768]{2,1,0:T(8,128)(2,1)} %gather_fusion) | data formatting | bytes 344064 | tf_op jit(solution)/shard_map/jit(_take)/gather | solution.py:36
  18.6 1.5 %copy_select_fusion = bf16[8,14,32,24]{3,0,2,1:T(8,128)(2,1)} fusion(bf16[8,14,32,24]{3,2,1,0:T(8,128)(2,1)S(1)} %reshape.147, pred[8]{0:T(512)(128)(4,1)S(1)} %and_reduce_fusion), kind=kLoop, calls=%fused_computation.6 | loop fusion | flops 86016 | bytes 344072 | tf_op jit(solution)/shard_map/jit(_take)/select_n | solution.py:36
  20.1 1.8 %gather_fusion.1 = bf16[8,8,14,24]{3,1,2,0:T(8,128)(2,1)S(1)} fusion(bf16[8,14,32,24]{3,0,2,1:T(8,128)(2,1)} %copy_select_fusion, s32[1024]{0:T(1024)S(1)} %pad_clamp_fusion), kind=kCustom, calls=%fused_computation.1 | custom fusion | bytes 86048 | tf_op jit(solution)/shard_map/jit(_take)/gather | solution.py:37
  21.9 0.1 broadcast_select_fusion
  22.1 6.0 %all-to-all-done = bf16[8,28,896]{2,1,0:T(8,128)(2,1)S(1)} async-done(((bf16[8,28,896]{2,1,0:T(8,128)(2,1)}), bf16[8,28,896]{2,1,0:T(8,128)(2,1)S(1)}, u32[]{:S(2)}, u32[]{:S(2)}) %all-to-all-start) | async-done | bytes 401440 | tf_op jit(solution)/shard_map/all_to_all | solution.py:25
  28.1 0.1 reshape.126
  28.2 0.5 %fusion.1 = bf16[224,768]{1,0:T(8,128)(2,1)S(1)} fusion(bf16[224,896]{1,0:T(8,128)(2,1)S(1)} %reshape.126, bf16[896,768]{1,0:T(8,128)(2,1)S(1)} %bitcast.47), kind=kOutput, calls=%fused_computation.5 | convolution fusion | flops 308453376 | bytes 2121728 | tf_op jit(solution)/shard_map/dot_general | solution.py:30
  28.7 0.1 reshape.127
  28.8 0.4 fusion
  29.2 14.9 %all_to_all.10 = bf16[8,24,768]{2,1,0:T(8,128)(2,1)S(1)} all-to-all(bf16[8,24,768]{2,1,0:T(8,128)(2,1)S(1)} %fusion), channel_id=1, replica_groups=mesh['z'=8,'xh'=2,'y'=4,'xl'=2,'c'=2] {'xh','y'}, dimensions={0} | all-to-all | bytes 589824 | tf_op jit(solution)/shard_map/all_to_all | solution.py:42
  44.2 0.7 %reshape.128 = f32[24,1,768]{2,1,0:T(1,128)} reshape(f32[24,768]{1,0:T(8,128)S(1)} %convert_reduce_fusion) | data formatting | bytes 147456 | tf_op jit(solution)/shard_map/reshape | solution.py:44
  (24 shorter events, 0.5 us)
Async XLA Ops:
  0.0 11.7 %copy-start.1 = (s32[64]{0:T(128)S(1)}, s32[64]{0:T(128)}, u32[]{:S(2)}) copy-start(s32[64]{0:T(128)} %param.6) | copy-start | bytes 772
  0.0 12.2 %copy-start.2 = (s32[64]{0:T(128)S(1)}, s32[64]{0:T(128)}, u32[]{:S(2)}) copy-start(s32[64]{0:T(128)} %param.7) | copy-start | bytes 772
  0.0 12.9 %collective-permute-start = (bf16[224,768]{1,0:T(8,128)(2,1)}, bf16[224,768]{1,0:T(8,128)(2,1)S(1)}, u32[]{:S(2)}, u32[]{:S(2)}) collective-permute-start(bf16[224,768]{1,0:T(8,128)(2,1)} %param.5), channel_id=1, source_target_pairs={{0,1},{1,0},{2,3},{3,2},{4,5},{5,4},{6,7},{7,6},{8,9},{9,8},{10,11... | collective-permute-start | bytes 1032200 | tf_op jit(solution)/shard_map/ppermute | solution.py:12
  0.0 12.7 %collective-permute-start.1 = (bf16[224,768]{1,0:T(8,128)(2,1)}, bf16[224,768]{1,0:T(8,128)(2,1)S(1)}, u32[]{:S(2)}, u32[]{:S(2)}) collective-permute-start(bf16[224,768]{1,0:T(8,128)(2,1)} %param.5), channel_id=1, source_target_pairs={{0,2},{2,0},{1,3},{3,1},{4,6},{6,4},{5,7},{7,5},{8,10},{10,8},{9,1... | collective-permute-start | bytes 1032200 | tf_op jit(solution)/shard_map/ppermute | solution.py:12
  2.4 10.3 %copy-start = (bf16[224,768]{1,0:T(8,128)(2,1)S(1)}, bf16[224,768]{1,0:T(8,128)(2,1)}, u32[]{:S(2)}) copy-start(bf16[224,768]{1,0:T(8,128)(2,1)} %param.5) | copy-start | bytes 1032196
  3.2 24.9 %all-to-all-start = ((bf16[8,28,896]{2,1,0:T(8,128)(2,1)}), bf16[8,28,896]{2,1,0:T(8,128)(2,1)S(1)}, u32[]{:S(2)}, u32[]{:S(2)}) async-start(bf16[8,28,896]{2,1,0:T(8,128)(2,1)} %broadcast_in_dim.50), calls=%async_computation | async-start | bytes 917504 | tf_op jit(solution)/shard_map/all_to_all | solution.py:25
  12.8 1.7 %collective-permute-start.2 = (bf16[224,768]{1,0:T(8,128)(2,1)S(1)}, bf16[224,768]{1,0:T(8,128)(2,1)S(1)}, u32[]{:S(2)}, u32[]{:S(2)}) collective-permute-start(bf16[224,768]{1,0:T(8,128)(2,1)S(1)} %collective-permute-done.1), channel_id=1, source_target_pairs={{0,1},{1,0},{2,3},{3,2},{4,5},{5,4},{6,7},{7,6},{8,9},{9,8},{10,11... | collective-permute-start | bytes 1032200 | tf_op jit(solution)/shard_map/ppermute | solution.py:12

commit v2 on v1

v2 whole, which is shorter than its diff:
```python
import functools

import jax
import jax.numpy as jnp
from jax import lax
from jax.experimental import pallas as pl
from jax.experimental.pallas import tpu as pltpu
from jax.sharding import Mesh, PartitionSpec as P


S1 = ("xh", "y")
S2 = ("z",)
OCC = ("xl", "c")
SIDE = 8


def swap(x, axis):
    return lax.ppermute(x, axis, [(0, 1), (1, 0)])


def hot_kernel(sblock, nocc, cut, pair_map, tile_table, own, full, row_pick, col_pick, mine, pairs, tiles, sems):
    nbf, nvirt = full.shape
    depth = own.shape[0]
    o = lax.axis_index("xl") * 2 + lax.axis_index("c")
    gets = [
        pltpu.make_async_copy(pair_map, pairs, sems.at[0]),
        pltpu.make_async_copy(tile_table, tiles, sems.at[1]),
        pltpu.make_async_copy(own, full.at[pl.ds(pl.multiple_of(o * depth, depth), depth), :], sems.at[2]),
    ]
    for g in gets:
        g.start()
    q = lax.axis_index("xh") * 4 + lax.axis_index("y")
    z = lax.axis_index("z")
    gets[0].wait()
    gets[1].wait()
    span = sblock * nocc
    k = SIDE * span
    r = lax.broadcasted_iota(jnp.int32, (k, 128), 0)
    goal = jnp.zeros((k, 128), jnp.int32)
    for s in range(SIDE):
        goal = jnp.where(r >= s * span, (pairs[z * SIDE + s] - s) * sblock, goal)
    goal = goal + r // nocc - lax.broadcasted_iota(jnp.int32, (k, 128), 1)
    for c in range(nbf // 128):
        row_pick[:, c * 128 : (c + 1) * 128] = (goal == 128 * c).astype(jnp.bfloat16)
    per = nvirt // cut
    lane = lax.broadcasted_iota(jnp.int32, (cut, 128), 1)
    line = lax.broadcasted_iota(jnp.int32, (cut, 128), 0)
    part = lax.broadcasted_iota(jnp.int32, (cut, k), 1) % nocc
    for s in range(SIDE):
        tile = tiles[s * SIDE + q]
        i = tile // per
        goal = (tile - i * per) * cut + line - lane
        at = pl.ds(s * cut, cut)
        for c in range(nvirt // 128):
            col_pick[at, c * 128 : (c + 1) * 128] = (goal == 128 * c).astype(jnp.bfloat16)
        mine[at, :] = (part == i).astype(jnp.float32)
    gets[2].wait()


def pick_kernel(twin, far, fartwin, row_pick, col_pick, mine, had, full, left):
    depth = twin.shape[0]
    o = lax.axis_index("xl") * 2 + lax.axis_index("c")
    for piece, k in ((twin, o ^ 1), (far, o ^ 2), (fartwin, o ^ 3)):
        full[pl.ds(pl.multiple_of(k * depth, depth), depth), :] = piece[...]
    rows = jnp.dot(row_pick[...], full[...], preferred_element_type=jnp.float32).astype(jnp.bfloat16)
    both = lax.dot_general(
        col_pick[...], rows, (((1,), (1,)), ((), ())), preferred_element_type=jnp.float32
    )
    left[...] = (both * mine[...]).astype(jnp.bfloat16)


def copies_kernel(rows, out, held, sem, sems):
    get = pltpu.make_async_copy(rows, held, sem)
    get.start()
    get.wait()
    puts = [pltpu.make_async_copy(held, out.at[k], sems.at[k]) for k in range(SIDE)]
    for c in puts:
        c.start()
    for c in puts:
        c.wait()


def mix_kernel(recv, full, left, part):
    half = jnp.dot(recv[...], full[...], preferred_element_type=jnp.float32).astype(jnp.bfloat16)
    part[...] = jnp.dot(left[...], half, preferred_element_type=jnp.float32).astype(jnp.bfloat16)


def layer(half_ints, coeffs, pair_map, tile_table):
    nocc, sblock, _, nbf = half_ints.shape
    nvirt = coeffs.shape[1]
    cut = nocc * nvirt // lax.axis_size(("z", "xh", "y"))
    vmem = pl.BlockSpec(memory_space=pltpu.VMEM)
    smem = pl.BlockSpec(memory_space=pltpu.SMEM)
    k = SIDE * nocc * sblock
    work = pl.CostEstimate(flops=2 * k * nvirt * (nbf + SIDE * cut), bytes_accessed=0, transcendentals=0)
    small = pltpu.CompilerParams(vmem_limit_bytes=16 << 20)
    far = swap(coeffs, "xl")
    nat = half_ints.transpose(1, 2, 0, 3)
    send = pl.pallas_call(
        copies_kernel,
        out_shape=pltpu.HBM((SIDE, *nat.shape), nat.dtype),
        in_specs=[pl.BlockSpec(memory_space=pltpu.HBM)],
        out_specs=pl.BlockSpec(memory_space=pltpu.HBM),
        scratch_shapes=[pltpu.VMEM(nat.shape, nat.dtype), pltpu.SemaphoreType.DMA, pltpu.SemaphoreType.DMA((SIDE,))],
        compiler_params=small,
        name="copies",
    )(pltpu.with_memory_space_constraint(nat, pltpu.HBM))
    recv = lax.all_to_all(send, S1, 0, 0, tiled=True)
    twin = swap(coeffs, "c")
    fartwin = swap(far, "c")
    hbm = pl.BlockSpec(memory_space=pltpu.HBM)
    own, row_pick, col_pick, mine = pl.pallas_call(
        functools.partial(hot_kernel, sblock, nocc, cut),
        out_shape=(
            jax.ShapeDtypeStruct((nbf, nvirt), jnp.bfloat16),
            jax.ShapeDtypeStruct((k, nbf), jnp.bfloat16),
            jax.ShapeDtypeStruct((SIDE * cut, nvirt), jnp.bfloat16),
            jax.ShapeDtypeStruct((SIDE * cut, k), jnp.float32),
        ),
        in_specs=[hbm] * 3,
        out_specs=(vmem,) * 4,
        scratch_shapes=[
            pltpu.SMEM(pair_map.shape, jnp.int32),
            pltpu.SMEM(tile_table.shape, jnp.int32),
            pltpu.SemaphoreType.DMA((3,)),
        ],
        cost_estimate=work,
        compiler_params=small,
        name="hot",
    )(*(pltpu.with_memory_space_constraint(v, pltpu.HBM) for v in (pair_map, tile_table, coeffs)))
    full, left = pl.pallas_call(
        pick_kernel,
        out_shape=(
            jax.ShapeDtypeStruct((nbf, nvirt), jnp.bfloat16),
            jax.ShapeDtypeStruct((SIDE * cut, k), jnp.bfloat16),
        ),
        in_specs=[vmem] * 7,
        out_specs=(vmem, vmem),
        input_output_aliases={6: 0},
        cost_estimate=work,
        compiler_params=small,
        name="pick",
    )(twin, far, fartwin, row_pick, col_pick, mine, own)
    part = pl.pallas_call(
        mix_kernel,
        out_shape=pltpu.VMEM((SIDE * cut, nvirt), jnp.bfloat16),
        in_specs=[vmem] * 3,
        out_specs=vmem,
        cost_estimate=work,
        compiler_params=small,
        name="mix",
    )(recv.reshape(k, nbf), full, left)
    got = lax.all_to_all(part.reshape(SIDE, cut, nvirt), S2, 0, 0, tiled=True)
    out = got.astype(jnp.float32).sum(0)
    return out.reshape(cut, 1, nvirt)


def solution(mesh):
    fine = Mesh(mesh.devices.reshape(8, 2, 4, 2, 2), ("z", "xh", "y", "xl", "c"))
    pair = ("z", "xh", "y")
    placed = (P(None, pair, OCC, None), P(OCC, None), P(), P())
    return jax.shard_map(layer, mesh=fine, in_specs=placed, out_specs=P(pair, OCC, None), check_vma=False)
```

time: 45.7 us -> 42.3 us (0.926)
  local copies, waits for them, and re-layouts: 8.86 us -> 3.43 us
  Pallas kernels: 0 us -> 4.29 us
  blocking collectives: 14.9 us -> 19.1 us
  other arithmetic: 2.25 us -> 0.04 us
  waiting for transfers between devices: 7.6 us -> 5.65 us
  starting transfers between devices: 10.1 us -> 9.09 us
  matrix products: 0.93 us -> 0 us
    gather x3 -> x0, local copies, waits for them, and re-layouts: 5.41 us -> none  [the longest x2 3.59 us: shards(): csel = jnp.take(full.reshape(64, sblock, nvirt), blocks, axis=0)]
    pallas_call x0 -> x4, Pallas kernels: none -> 4.29 us  [the longest x1 1.63 us: layer(): pl.pallas_call(copies_kernel, out_shape=pltpu.HBM((SIDE, *nat.shape), nat...]
    all_to_all x1, blocking collectives: 14.9 us -> 19.1 us  [layer(): got = lax.all_to_all(part.reshape(SIDE, cut, nvirt), S2, 0, 0, tiled=True)]
    select_n x5 -> x0, other arithmetic: 1.93 us -> none  [the longest x2 1.71 us: shards(): csel = jnp.take(full.reshape(64, sblock, nvirt), blocks, axis=0)]
    ppermute x3, waiting for transfers between devices: 1.56 us -> 0.01 us  [swap(): return lax.ppermute(x, axis, [(0, 1), (1, 0)])]
    all_to_all x1, starting transfers between devices: 8.47 us -> 7.09 us  [layer(): recv = lax.all_to_all(send, S1, 0, 0, tiled=True)]
    dot_general x2 -> x0, matrix products: 0.93 us -> none  [the longest x1 0.52 us: shards(): jnp.dot(recv.reshape(-1, nbf), full, preferred_element_type=jnp.float32)]
    broadcast_in_dim x2 -> x0, local copies, waits for them, and re-layouts: 0.9 us -> none  [the longest x1 0.81 us: shards(): send = jnp.broadcast_to(nat, (8, *nat.shape))]
  transfers between devices with their start and end apart: 4 -> 4, of which waited for: 2 -> 1; matrix products, arithmetic and copies ran while one was open for 23% -> 3% of each run, Pallas kernels for 0% -> 6%
where the time goes in v2:
time: 42.3 us; the launch traced here: 41.7 us
  blocking collectives  19.1 us (45%)
  starting transfers between devices  9.09 us (21%)
  waiting for transfers between devices  5.65 us (13%)
  Pallas kernels  4.29 us (10%)
  local copies, waits for them, and re-layouts  3.43 us (8%)
    all_to_all x1, blocking collectives, layer(): got = lax.all_to_all(part.reshape(SIDE, cut, nvirt), S2, 0, 0, tiled=True)  19.1 us
    all_to_all x1, starting transfers between devices, layer(): recv = lax.all_to_all(send, S1, 0, 0, tiled=True)  7.09 us
    all_to_all x1, waiting for transfers between devices, layer(): recv = lax.all_to_all(send, S1, 0, 0, tiled=True)  5.64 us
    ppermute x3, starting transfers between devices, swap(): return lax.ppermute(x, axis, [(0, 1), (1, 0)])  2 us
    pallas_call x1, Pallas kernels, layer(): pl.pallas_call(copies_kernel, out_shape=pltpu.HBM((SIDE, *nat.shape), nat...  1.63 us
    unnamed x4, local copies, waits for them, and re-layouts  1.6 us
    reshape x1, local copies, waits for them, and re-layouts, layer(): recv.reshape(k, nbf)  1.15 us
    pallas_call x1, Pallas kernels, layer(): pl.pallas_call(functools.partial(hot_kernel, sblock, nocc, cut), out_shap...  1 us
  transfers between devices with their start and end apart: 4, of which 1 were waited for; matrix products, arithmetic and copies ran while one was open for 3% of the time, Pallas kernels for 6%

profile of v2, /device:TPU:8, one launch (start us, length us, event | category | flops | bytes accessed | tf_op | source)
XLA Modules:
  0.0 41.7 jit_solution(1658370638940335847)
XLA Ops:
  0.0 1.5 %collective-permute-start.1 = (bf16[224,768]{1,0:T(8,128)(2,1)}, bf16[224,768]{1,0:T(8,128)(2,1)S(1)}, u32[]{:S(2)}, u32[]{:S(2)}) collective-permute-start(bf16[224,768]{1,0:T(8,128)(2,1)} %own.1), channel_id=1, source_target_pairs={{0,2},{2,0},{1,3},{3,1},{4,6},{6,4},{5,7},{7,5},{8,10},{10,8},{9,1... | collective-permute-start | bytes 1032200 | tf_op jit(solution)/shard_map/ppermute | solution.py:18
  1.5 1.6 %copies.1 = bf16[8,14,1,2,896]{4,3,2,1,0:T(2,128)(2,1)} custom-call(bf16[14,1,2,896]{3,2,1,0:T(2,128)(2,1)} %bitcast.3), custom_call_target="tpu_custom_call" | custom-call | tf_op jit(solution)/shard_map/copies/pallas_call | solution.py:99
  3.1 7.1 %all-to-all-start = ((bf16[8,14,1,2,896]{4,3,2,1,0:T(2,128)(2,1)}), bf16[8,14,1,2,896]{4,3,2,1,0:T(2,128)(2,1)}, u32[]{:S(2)}, u32[]{:S(2)}) async-start(bf16[8,14,1,2,896]{4,3,2,1,0:T(2,128)(2,1)} %copies.1), calls=%async_computation | async-start | bytes 802816 | tf_op jit(solution)/shard_map/all_to_all | solution.py:108
  10.2 0.0 collective-permute-start
  10.2 0.0 collective-permute-done.1.far
  10.2 0.5 %collective-permute-start.2 = (bf16[224,768]{1,0:T(8,128)(2,1)S(1)}, bf16[224,768]{1,0:T(8,128)(2,1)S(1)}, u32[]{:S(2)}, u32[]{:S(2)}) collective-permute-start(bf16[224,768]{1,0:T(8,128)(2,1)S(1)} %collective-permute-done.1.far), channel_id=1, source_target_pairs={{0,1},{1,0},{2,3},{3,2},{4,5},{5,4},{6,7},{7,6},{8,9},{9,8},{10,11... | collective-permute-start | bytes 1032200 | tf_op jit(solution)/shard_map/ppermute | solution.py:18
  10.7 1.0 %hot.1 = (bf16[896,768]{1,0:T(8,128)(2,1)S(1)}, bf16[224,896]{1,0:T(8,128)(2,1)S(1)}, bf16[192,768]{1,0:T(8,128)(2,1)S(1)}, f32[192,224]{1,0:T(8,128)S(1)}) custom-call(s32[64]{0:T(128)} %pair_map.1, s32[64]{0:T(128)} %tile_table.1, bf16[224,768]{1,0:T(8,128)(2,1)} %own.1), custom_call_target="tpu_custom_call" | custom-call | flops 374341632 | tf_op jit(solution)/shard_map/hot/pallas_call | solution.py:112
  11.8 0.0 copy-start
  11.8 0.7 %copy-done = f32[192,224]{1,0:T(8,128)} copy-done((f32[192,224]{1,0:T(8,128)}, f32[192,224]{1,0:T(8,128)S(1)}, u32[]{:S(2)}) %copy-start) | copy-done | bytes 172056
  12.4 5.6 %all-to-all-done = bf16[8,14,1,2,896]{4,3,2,1,0:T(2,128)(2,1)} async-done(((bf16[8,14,1,2,896]{4,3,2,1,0:T(2,128)(2,1)}), bf16[8,14,1,2,896]{4,3,2,1,0:T(2,128)(2,1)}, u32[]{:S(2)}, u32[]{:S(2)}) %all-to-all-start) | async-done | bytes 401440 | tf_op jit(solution)/shard_map/all_to_all | solution.py:108
  18.1 1.1 %reshape.9.recv = bf16[224,896]{1,0:T(8,128)(2,1)S(1)} reshape(bf16[8,14,1,2,896]{4,3,2,1,0:T(2,128)(2,1)} %all-to-all-done) | data formatting | bytes 802816 | tf_op jit(solution)/shard_map/reshape | solution.py:152
  19.2 0.0 collective-permute-done.twin
  19.2 0.0 collective-permute-done.2.fartwin
  19.3 0.0 copy-start.1
  19.3 0.9 %copy-done.1 = f32[192,224]{1,0:T(8,128)S(1)} copy-done((f32[192,224]{1,0:T(8,128)S(1)}, f32[192,224]{1,0:T(8,128)}, u32[]{:S(2)}) %copy-start.1) | copy-done | bytes 172056
  20.2 0.9 %pick.1 = (bf16[896,768]{1,0:T(8,128)(2,1)S(1)}, bf16[192,224]{1,0:T(8,128)(2,1)S(1)}) custom-call(bf16[224,768]{1,0:T(8,128)(2,1)S(1)} %collective-permute-done.twin, bf16[224,768]{1,0:T(8,128)(2,1)S(1)} %collective-permute-done.1.far, bf16[224,768]{1,0:T(8,128)(2,1)S(1)} %collective-permute-done.2.fartwin, ...), custom_call_target="tpu_custom_call", output_to_operand_aliasing={{0}: (6, {})} | custom-call | flops 374341632 | tf_op jit(solution)/shard_map/pick/pallas_call | solution.py:131
  21.1 0.8 %mix.1 = bf16[192,768]{1,0:T(8,128)(2,1)S(1)} custom-call(bf16[224,896]{1,0:T(8,128)(2,1)S(1)} %reshape.9.recv, bf16[896,768]{1,0:T(8,128)(2,1)S(1)} %get-tuple-element.15.full, bf16[192,224]{1,0:T(8,128)(2,1)S(1)} %get-tuple-element.16.left), custom_call_target="tpu_custom_call" | custom-call | flops 374341632 | tf_op jit(solution)/shard_map/mix/pallas_call | solution.py:144
  21.9 19.1 %all_to_all.10 = bf16[8,24,768]{2,1,0:T(8,128)(2,1)S(1)} all-to-all(bf16[8,24,768]{2,1,0:T(8,128)(2,1)S(1)} %bitcast.2), channel_id=1, replica_groups=mesh['z'=8,'xh'=2,'y'=4,'xl'=2,'c'=2] {'z'}, dimensions={0} | all-to-all | bytes 589824 | tf_op jit(solution)/shard_map/all_to_all | solution.py:153
  41.0 0.7 %reshape.11 = f32[24,1,768]{2,1,0:T(1,128)} reshape(f32[24,768]{1,0:T(8,128)S(1)} %convert_reduce_fusion) | data formatting | bytes 147456 | tf_op jit(solution)/shard_map/reshape | solution.py:155
  (1 shorter events, 0.0 us)
Async XLA Ops:
  0.0 10.2 %collective-permute-start.1 = (bf16[224,768]{1,0:T(8,128)(2,1)}, bf16[224,768]{1,0:T(8,128)(2,1)S(1)}, u32[]{:S(2)}, u32[]{:S(2)}) collective-permute-start(bf16[224,768]{1,0:T(8,128)(2,1)} %own.1), channel_id=1, source_target_pairs={{0,2},{2,0},{1,3},{3,1},{4,6},{6,4},{5,7},{7,5},{8,10},{10,8},{9,1... | collective-permute-start | bytes 1032200 | tf_op jit(solution)/shard_map/ppermute | solution.py:18
  3.1 14.9 %all-to-all-start = ((bf16[8,14,1,2,896]{4,3,2,1,0:T(2,128)(2,1)}), bf16[8,14,1,2,896]{4,3,2,1,0:T(2,128)(2,1)}, u32[]{:S(2)}, u32[]{:S(2)}) async-start(bf16[8,14,1,2,896]{4,3,2,1,0:T(2,128)(2,1)} %copies.1), calls=%async_computation | async-start | bytes 802816 | tf_op jit(solution)/shard_map/all_to_all | solution.py:108
  10.2 9.0 %collective-permute-start = (bf16[224,768]{1,0:T(8,128)(2,1)}, bf16[224,768]{1,0:T(8,128)(2,1)S(1)}, u32[]{:S(2)}, u32[]{:S(2)}) collective-permute-start(bf16[224,768]{1,0:T(8,128)(2,1)} %own.1), channel_id=1, source_target_pairs={{0,1},{1,0},{2,3},{3,2},{4,5},{5,4},{6,7},{7,6},{8,9},{9,8},{10,11... | collective-permute-start | bytes 1032200 | tf_op jit(solution)/shard_map/ppermute | solution.py:18
  10.2 9.0 %collective-permute-start.2 = (bf16[224,768]{1,0:T(8,128)(2,1)S(1)}, bf16[224,768]{1,0:T(8,128)(2,1)S(1)}, u32[]{:S(2)}, u32[]{:S(2)}) collective-permute-start(bf16[224,768]{1,0:T(8,128)(2,1)S(1)} %collective-permute-done.1.far), channel_id=1, source_target_pairs={{0,1},{1,0},{2,3},{3,2},{4,5},{5,4},{6,7},{7,6},{8,9},{9,8},{10,11... | collective-permute-start | bytes 1032200 | tf_op jit(solution)/shard_map/ppermute | solution.py:18
  11.8 0.7 %copy-start = (f32[192,224]{1,0:T(8,128)}, f32[192,224]{1,0:T(8,128)S(1)}, u32[]{:S(2)}) copy-start(f32[192,224]{1,0:T(8,128)S(1)} %get-tuple-element.13.mine) | copy-start | bytes 516100
  19.3 0.9 %copy-start.1 = (f32[192,224]{1,0:T(8,128)S(1)}, f32[192,224]{1,0:T(8,128)}, u32[]{:S(2)}) copy-start(f32[192,224]{1,0:T(8,128)} %copy-done) | copy-start | bytes 516100

commit v3 on v2

--- a/solution.py
+++ b/solution.py
@@ -8,10 +8,15 @@
 from jax.sharding import Mesh, PartitionSpec as P
 
 
-S1 = ("xh", "y")
-S2 = ("z",)
+PAIR = ("z", "xh", "y")
+PLANE_ORDER = (5, 6, 7, 0, 1, 2, 3, 4)
+LINE_ORDER = (5, 1, 6, 2, 7, 3, 0, 4)
 OCC = ("xl", "c")
 SIDE = 8
+
+
+def exchange(x, groups):
+    return lax.all_to_all(x, PAIR, 0, 0, tiled=True, axis_index_groups=groups)
 
 
 def swap(x, axis):
@@ -38,7 +43,7 @@
     r = lax.broadcasted_iota(jnp.int32, (k, 128), 0)
     goal = jnp.zeros((k, 128), jnp.int32)
     for s in range(SIDE):
-        goal = jnp.where(r >= s * span, (pairs[z * SIDE + s] - s) * sblock, goal)
+        goal = jnp.where(r >= s * span, (pairs[z * SIDE + PLANE_ORDER[s]] - s) * sblock, goal)
     goal = goal + r // nocc - lax.broadcasted_iota(jnp.int32, (k, 128), 1)
     for c in range(nbf // 128):
         row_pick[:, c * 128 : (c + 1) * 128] = (goal == 128 * c).astype(jnp.bfloat16)
@@ -47,7 +52,7 @@
     line = lax.broadcasted_iota(jnp.int32, (cut, 128), 0)
     part = lax.broadcasted_iota(jnp.int32, (cut, k), 1) % nocc
     for s in range(SIDE):
-        tile = tiles[s * SIDE + q]
+        tile = tiles[LINE_ORDER[s] * SIDE + q]
         i = tile // per
         goal = (tile - i * per) * cut + line - lane
         at = pl.ds(s * cut, cut)
@@ -88,7 +93,7 @@
 def layer(half_ints, coeffs, pair_map, tile_table):
     nocc, sblock, _, nbf = half_ints.shape
     nvirt = coeffs.shape[1]
-    cut = nocc * nvirt // lax.axis_size(("z", "xh", "y"))
+    cut = nocc * nvirt // lax.axis_size(PAIR)
     vmem = pl.BlockSpec(memory_space=pltpu.VMEM)
     smem = pl.BlockSpec(memory_space=pltpu.SMEM)
     k = SIDE * nocc * sblock
@@ -105,7 +110,7 @@
         compiler_params=small,
         name="copies",
     )(pltpu.with_memory_space_constraint(nat, pltpu.HBM))
-    recv = lax.all_to_all(send, S1, 0, 0, tiled=True)
+    recv = exchange(send, [[z * SIDE + q for q in PLANE_ORDER] for z in range(SIDE)])
     twin = swap(coeffs, "c")
     fartwin = swap(far, "c")
     hbm = pl.BlockSpec(memory_space=pltpu.HBM)
@@ -150,13 +155,12 @@
         compiler_params=small,
         name="mix",
     )(recv.reshape(k, nbf), full, left)
-    got = lax.all_to_all(part.reshape(SIDE, cut, nvirt), S2, 0, 0, tiled=True)
+    got = exchange(part.reshape(SIDE, cut, nvirt), [[z * SIDE + q for z in LINE_ORDER] for q in range(SIDE)])
     out = got.astype(jnp.float32).sum(0)
     return out.reshape(cut, 1, nvirt)
 
 
 def solution(mesh):
     fine = Mesh(mesh.devices.reshape(8, 2, 4, 2, 2), ("z", "xh", "y", "xl", "c"))
-    pair = ("z", "xh", "y")
-    placed = (P(None, pair, OCC, None), P(OCC, None), P(), P())
-    return jax.shard_map(layer, mesh=fine, in_specs=placed, out_specs=P(pair, OCC, None), check_vma=False)
+    placed = (P(None, PAIR, OCC, None), P(OCC, None), P(), P())
+    return jax.shard_map(layer, mesh=fine, in_specs=placed, out_specs=P(PAIR, OCC, None), check_vma=False)

time: 42.3 us -> 39.3 us (0.929)
  blocking collectives: 19.1 us -> 16.9 us
  starting transfers between devices: 9.09 us -> 8.6 us
    all_to_all x1, blocking collectives: 19.1 us -> 16.9 us  [exchange(): return lax.all_to_all(x, PAIR, 0, 0, tiled=True, axis_index_groups=groups)]
  transfers between devices with their start and end apart: 4 -> 4, of which waited for: 1 -> 2; matrix products, arithmetic and copies ran while one was open for 3% -> 3% of each run, Pallas kernels for 6% -> 7%
where the time goes in v3:
time: 39.3 us; the launch traced here: 39 us
  blocking collectives  16.9 us (43%)
  starting transfers between devices  8.6 us (22%)
  waiting for transfers between devices  5.64 us (14%)
  Pallas kernels  4.28 us (11%)
  local copies, waits for them, and re-layouts  3.43 us (9%)
    all_to_all x1, blocking collectives, exchange(): return lax.all_to_all(x, PAIR, 0, 0, tiled=True, axis_index_groups=groups)  16.9 us
    all_to_all x1, starting transfers between devices, exchange(): return lax.all_to_all(x, PAIR, 0, 0, tiled=True, axis_index_groups=groups)  6.73 us
    all_to_all x1, waiting for transfers between devices, exchange(): return lax.all_to_all(x, PAIR, 0, 0, tiled=True, axis_index_groups=groups)  5.49 us
    ppermute x3, starting transfers between devices, swap(): return lax.ppermute(x, axis, [(0, 1), (1, 0)])  1.86 us
    pallas_call x1, Pallas kernels, layer(): pl.pallas_call(copies_kernel, out_shape=pltpu.HBM((SIDE, *nat.shape), nat...  1.63 us
    unnamed x4, local copies, waits for them, and re-layouts  1.6 us
    reshape x1, local copies, waits for them, and re-layouts, layer(): recv.reshape(k, nbf)  1.15 us
    pallas_call x1, Pallas kernels, layer(): pl.pallas_call(functools.partial(hot_kernel, sblock, nocc, cut), out_shap...  1 us
  transfers between devices with their start and end apart: 4, of which 2 were waited for; matrix products, arithmetic and copies ran while one was open for 3% of the time, Pallas kernels for 7%

profile of v3, /device:TPU:8, one launch (start us, length us, event | category | flops | bytes accessed | tf_op | source)
XLA Modules:
  0.0 39.0 jit_solution(1842630981111288225)
XLA Ops:
  0.0 1.5 %collective-permute-start.1 = (bf16[224,768]{1,0:T(8,128)(2,1)}, bf16[224,768]{1,0:T(8,128)(2,1)S(1)}, u32[]{:S(2)}, u32[]{:S(2)}) collective-permute-start(bf16[224,768]{1,0:T(8,128)(2,1)} %own.1), channel_id=1, source_target_pairs={{0,2},{2,0},{1,3},{3,1},{4,6},{6,4},{5,7},{7,5},{8,10},{10,8},{9,1... | collective-permute-start | bytes 1032200 | tf_op jit(solution)/shard_map/ppermute | solution.py:23
  1.5 1.6 %copies.1 = bf16[8,14,1,2,896]{4,3,2,1,0:T(2,128)(2,1)} custom-call(bf16[14,1,2,896]{3,2,1,0:T(2,128)(2,1)} %bitcast.3), custom_call_target="tpu_custom_call" | custom-call | tf_op jit(solution)/shard_map/copies/pallas_call | solution.py:104
  3.1 6.7 %all-to-all-start = ((bf16[8,14,1,2,896]{4,3,2,1,0:T(2,128)(2,1)}), bf16[8,14,1,2,896]{4,3,2,1,0:T(2,128)(2,1)}, u32[]{:S(2)}, u32[]{:S(2)}) async-start(bf16[8,14,1,2,896]{4,3,2,1,0:T(2,128)(2,1)} %copies.1), calls=%async_computation | async-start | bytes 802816 | tf_op jit(solution)/shard_map/all_to_all | solution.py:19
  9.9 0.0 collective-permute-start
  9.9 0.1 collective-permute-done.1.far
  10.0 0.4 collective-permute-start.2
  10.4 1.0 %hot.1 = (bf16[896,768]{1,0:T(8,128)(2,1)S(1)}, bf16[224,896]{1,0:T(8,128)(2,1)S(1)}, bf16[192,768]{1,0:T(8,128)(2,1)S(1)}, f32[192,224]{1,0:T(8,128)S(1)}) custom-call(s32[64]{0:T(128)} %pair_map.1, s32[64]{0:T(128)} %tile_table.1, bf16[224,768]{1,0:T(8,128)(2,1)} %own.1), custom_call_target="tpu_custom_call" | custom-call | flops 374341632 | tf_op jit(solution)/shard_map/hot/pallas_call | solution.py:117
  11.4 0.0 copy-start
  11.4 0.7 %copy-done = f32[192,224]{1,0:T(8,128)} copy-done((f32[192,224]{1,0:T(8,128)}, f32[192,224]{1,0:T(8,128)S(1)}, u32[]{:S(2)}) %copy-start) | copy-done | bytes 172056
  12.1 5.5 %all-to-all-done = bf16[8,14,1,2,896]{4,3,2,1,0:T(2,128)(2,1)} async-done(((bf16[8,14,1,2,896]{4,3,2,1,0:T(2,128)(2,1)}), bf16[8,14,1,2,896]{4,3,2,1,0:T(2,128)(2,1)}, u32[]{:S(2)}, u32[]{:S(2)}) %all-to-all-start) | async-done | bytes 401440 | tf_op jit(solution)/shard_map/all_to_all | solution.py:19
  17.6 1.1 %reshape.9.recv = bf16[224,896]{1,0:T(8,128)(2,1)S(1)} reshape(bf16[8,14,1,2,896]{4,3,2,1,0:T(2,128)(2,1)} %all-to-all-done) | data formatting | bytes 802816 | tf_op jit(solution)/shard_map/reshape | solution.py:157
  18.7 0.0 collective-permute-done.twin
  18.7 0.0 collective-permute-done.2.fartwin
  18.7 0.0 copy-start.1
  18.8 0.9 %copy-done.1 = f32[192,224]{1,0:T(8,128)S(1)} copy-done((f32[192,224]{1,0:T(8,128)S(1)}, f32[192,224]{1,0:T(8,128)}, u32[]{:S(2)}) %copy-start.1) | copy-done | bytes 172056
  19.7 0.9 %pick.1 = (bf16[896,768]{1,0:T(8,128)(2,1)S(1)}, bf16[192,224]{1,0:T(8,128)(2,1)S(1)}) custom-call(bf16[224,768]{1,0:T(8,128)(2,1)S(1)} %collective-permute-done.twin, bf16[224,768]{1,0:T(8,128)(2,1)S(1)} %collective-permute-done.1.far, bf16[224,768]{1,0:T(8,128)(2,1)S(1)} %collective-permute-done.2.fartwin, ...), custom_call_target="tpu_custom_call", output_to_operand_aliasing={{0}: (6, {})} | custom-call | flops 374341632 | tf_op jit(solution)/shard_map/pick/pallas_call | solution.py:136
  20.6 0.8 %mix.1 = bf16[192,768]{1,0:T(8,128)(2,1)S(1)} custom-call(bf16[224,896]{1,0:T(8,128)(2,1)S(1)} %reshape.9.recv, bf16[896,768]{1,0:T(8,128)(2,1)S(1)} %get-tuple-element.15.full, bf16[192,224]{1,0:T(8,128)(2,1)S(1)} %get-tuple-element.16.left), custom_call_target="tpu_custom_call" | custom-call | flops 374341632 | tf_op jit(solution)/shard_map/mix/pallas_call | solution.py:149
  21.3 16.9 %all_to_all.10 = bf16[8,24,768]{2,1,0:T(8,128)(2,1)S(1)} all-to-all(bf16[8,24,768]{2,1,0:T(8,128)(2,1)S(1)} %bitcast.2), channel_id=1, replica_groups={{160,32,192,64,224,96,0,128},{164,36,196,68,228,100,4,132},{168,40,200,..., dimensions={0} | all-to-all | bytes 589824 | tf_op jit(solution)/shard_map/all_to_all | solution.py:19
  38.3 0.7 %reshape.11 = f32[24,1,768]{2,1,0:T(1,128)} reshape(f32[24,768]{1,0:T(8,128)S(1)} %convert_reduce_fusion) | data formatting | bytes 147456 | tf_op jit(solution)/shard_map/reshape | solution.py:160
  (1 shorter events, 0.0 us)
Async XLA Ops:
  0.0 10.0 %collective-permute-start.1 = (bf16[224,768]{1,0:T(8,128)(2,1)}, bf16[224,768]{1,0:T(8,128)(2,1)S(1)}, u32[]{:S(2)}, u32[]{:S(2)}) collective-permute-start(bf16[224,768]{1,0:T(8,128)(2,1)} %own.1), channel_id=1, source_target_pairs={{0,2},{2,0},{1,3},{3,1},{4,6},{6,4},{5,7},{7,5},{8,10},{10,8},{9,1... | collective-permute-start | bytes 1032200 | tf_op jit(solution)/shard_map/ppermute | solution.py:23
  3.1 14.4 %all-to-all-start = ((bf16[8,14,1,2,896]{4,3,2,1,0:T(2,128)(2,1)}), bf16[8,14,1,2,896]{4,3,2,1,0:T(2,128)(2,1)}, u32[]{:S(2)}, u32[]{:S(2)}) async-start(bf16[8,14,1,2,896]{4,3,2,1,0:T(2,128)(2,1)} %copies.1), calls=%async_computation | async-start | bytes 802816 | tf_op jit(solution)/shard_map/all_to_all | solution.py:19
  9.9 8.9 %collective-permute-start = (bf16[224,768]{1,0:T(8,128)(2,1)}, bf16[224,768]{1,0:T(8,128)(2,1)S(1)}, u32[]{:S(2)}, u32[]{:S(2)}) collective-permute-start(bf16[224,768]{1,0:T(8,128)(2,1)} %own.1), channel_id=1, source_target_pairs={{0,1},{1,0},{2,3},{3,2},{4,5},{5,4},{6,7},{7,6},{8,9},{9,8},{10,11... | collective-permute-start | bytes 1032200 | tf_op jit(solution)/shard_map/ppermute | solution.py:23
  10.0 8.7 %collective-permute-start.2 = (bf16[224,768]{1,0:T(8,128)(2,1)S(1)}, bf16[224,768]{1,0:T(8,128)(2,1)S(1)}, u32[]{:S(2)}, u32[]{:S(2)}) collective-permute-start(bf16[224,768]{1,0:T(8,128)(2,1)S(1)} %collective-permute-done.1.far), channel_id=1, source_target_pairs={{0,1},{1,0},{2,3},{3,2},{4,5},{5,4},{6,7},{7,6},{8,9},{9,8},{10,11... | collective-permute-start | bytes 1032200 | tf_op jit(solution)/shard_map/ppermute | solution.py:23
  11.4 0.7 %copy-start = (f32[192,224]{1,0:T(8,128)}, f32[192,224]{1,0:T(8,128)S(1)}, u32[]{:S(2)}) copy-start(f32[192,224]{1,0:T(8,128)S(1)} %get-tuple-element.13.mine) | copy-start | bytes 516100
  18.7 0.9 %copy-start.1 = (f32[192,224]{1,0:T(8,128)S(1)}, f32[192,224]{1,0:T(8,128)}, u32[]{:S(2)}) copy-start(f32[192,224]{1,0:T(8,128)} %copy-done) | copy-start | bytes 516100

commit v4 on v3

--- a/solution.py
+++ b/solution.py
@@ -9,14 +9,21 @@
 
 
 PAIR = ("z", "xh", "y")
+PLANE_FIRST = 0
 PLANE_ORDER = (5, 6, 7, 0, 1, 2, 3, 4)
 LINE_ORDER = (5, 1, 6, 2, 7, 3, 0, 4)
 OCC = ("xl", "c")
 SIDE = 8
 
 
-def exchange(x, groups):
-    return lax.all_to_all(x, PAIR, 0, 0, tiled=True, axis_index_groups=groups)
+def exchange(x, plane_core):
+    groups = []
+    for fixed in range(SIDE):
+        for xl in range(2):
+            plane = [(fixed * SIDE + q) * 4 + xl * 2 + plane_core for q in PLANE_ORDER]
+            line = [(z * SIDE + fixed) * 4 + xl * 2 + 1 - plane_core for z in LINE_ORDER]
+            groups += [plane, line]
+    return lax.all_to_all(x, PAIR + OCC, 0, 0, tiled=True, axis_index_groups=groups)
 
 
 def swap(x, axis):
@@ -36,6 +43,7 @@
         g.start()
     q = lax.axis_index("xh") * 4 + lax.axis_index("y")
     z = lax.axis_index("z")
+    plane_first = lax.axis_index("c") == PLANE_FIRST
     gets[0].wait()
     gets[1].wait()
     span = sblock * nocc
@@ -43,7 +51,8 @@
     r = lax.broadcasted_iota(jnp.int32, (k, 128), 0)
     goal = jnp.zeros((k, 128), jnp.int32)
     for s in range(SIDE):
-        goal = jnp.where(r >= s * span, (pairs[z * SIDE + PLANE_ORDER[s]] - s) * sblock, goal)
+        source = jnp.where(plane_first, z * SIDE + PLANE_ORDER[s], LINE_ORDER[s] * SIDE + q)
+        goal = jnp.where(r >= s * span, (pairs[source] - s) * sblock, goal)
     goal = goal + r // nocc - lax.broadcasted_iota(jnp.int32, (k, 128), 1)
     for c in range(nbf // 128):
         row_pick[:, c * 128 : (c + 1) * 128] = (goal == 128 * c).astype(jnp.bfloat16)
@@ -52,7 +61,7 @@
     line = lax.broadcasted_iota(jnp.int32, (cut, 128), 0)
     part = lax.broadcasted_iota(jnp.int32, (cut, k), 1) % nocc
     for s in range(SIDE):
-        tile = tiles[LINE_ORDER[s] * SIDE + q]
+        tile = tiles[jnp.where(plane_first, LINE_ORDER[s] * SIDE + q, z * SIDE + PLANE_ORDER[s])]
         i = tile // per
         goal = (tile - i * per) * cut + line - lane
         at = pl.ds(s * cut, cut)
@@ -110,7 +119,7 @@
         compiler_params=small,
         name="copies",
     )(pltpu.with_memory_space_constraint(nat, pltpu.HBM))
-    recv = exchange(send, [[z * SIDE + q for q in PLANE_ORDER] for z in range(SIDE)])
+    recv = exchange(send, PLANE_FIRST)
     twin = swap(coeffs, "c")
     fartwin = swap(far, "c")
     hbm = pl.BlockSpec(memory_space=pltpu.HBM)
@@ -155,7 +164,7 @@
         compiler_params=small,
         name="mix",
     )(recv.reshape(k, nbf), full, left)
-    got = exchange(part.reshape(SIDE, cut, nvirt), [[z * SIDE + q for z in LINE_ORDER] for q in range(SIDE)])
+    got = exchange(part.reshape(SIDE, cut, nvirt), 1 - PLANE_FIRST)
     out = got.astype(jnp.float32).sum(0)
     return out.reshape(cut, 1, nvirt)
 

time: 39.3 us -> 34.2 us (0.87)
  waiting for transfers between devices: 5.64 us -> 1.99 us
  local copies, waits for them, and re-layouts: 3.43 us -> 0.84 us
  starting transfers between devices: 8.6 us -> 11 us
  blocking collectives: 16.9 us -> 15.6 us
    all_to_all x1, waiting for transfers between devices: 5.49 us -> 1.12 us  [exchange(): lax.all_to_all(x, PAIR + OCC, 0, 0, tiled=True, axis_index_groups=groups)]
    ppermute x3, starting transfers between devices: 1.86 us -> 4.46 us  [swap(): return lax.ppermute(x, axis, [(0, 1), (1, 0)])]
    unnamed x4 -> x0, local copies, waits for them, and re-layouts: 1.6 us -> none
    all_to_all x1, blocking collectives: 16.9 us -> 15.6 us  [exchange(): lax.all_to_all(x, PAIR + OCC, 0, 0, tiled=True, axis_index_groups=groups)]
    reshape x1, local copies, waits for them, and re-layouts: 1.15 us -> 0.15 us  [layer(): recv.reshape(k, nbf)]
    ppermute x3, waiting for transfers between devices: 0.15 us -> 0.88 us  [swap(): return lax.ppermute(x, axis, [(0, 1), (1, 0)])]
  transfers between devices with their start and end apart: 4 -> 4, of which waited for: 2 -> 3; matrix products, arithmetic and copies ran while one was open for 3% -> 0% of each run, Pallas kernels for 7% -> 10%
where the time goes in v4:
time: 34.2 us; the launch traced here: 33.8 us
  blocking collectives  15.6 us (46%)
  starting transfers between devices  11 us (32%)
  Pallas kernels  4.28 us (13%)
  waiting for transfers between devices  1.99 us (6%)
  local copies, waits for them, and re-layouts  0.84 us (2%)
    all_to_all x1, blocking collectives, exchange(): lax.all_to_all(x, PAIR + OCC, 0, 0, tiled=True, axis_index_groups=groups)  15.6 us
    all_to_all x1, starting transfers between devices, exchange(): lax.all_to_all(x, PAIR + OCC, 0, 0, tiled=True, axis_index_groups=groups)  6.55 us
    ppermute x3, starting transfers between devices, swap(): return lax.ppermute(x, axis, [(0, 1), (1, 0)])  4.46 us
    pallas_call x1, Pallas kernels, layer(): pl.pallas_call(copies_kernel, out_shape=pltpu.HBM((SIDE, *nat.shape), nat...  1.63 us
    all_to_all x1, waiting for transfers between devices, exchange(): lax.all_to_all(x, PAIR + OCC, 0, 0, tiled=True, axis_index_groups=groups)  1.12 us
    pallas_call x1, Pallas kernels, layer(): pl.pallas_call(functools.partial(hot_kernel, sblock, nocc, cut), out_shap...  1 us
    pallas_call x1, Pallas kernels, layer(): pl.pallas_call(pick_kernel, out_shape=(jax.ShapeDtypeStruct((nbf, nvirt),...  0.88 us
    ppermute x3, waiting for transfers between devices, swap(): return lax.ppermute(x, axis, [(0, 1), (1, 0)])  0.88 us
  transfers between devices with their start and end apart: 4, of which 3 were waited for; matrix products, arithmetic and copies ran while one was open for 0% of the time, Pallas kernels for 10%

profile of v4, /device:TPU:8, one launch (start us, length us, event | category | flops | bytes accessed | tf_op | source)
XLA Modules:
  0.0 33.8 jit_solution(15226281742828891663)
XLA Ops:
  0.0 1.5 %collective-permute-start.1 = (bf16[224,768]{1,0:T(8,128)(2,1)}, bf16[224,768]{1,0:T(8,128)(2,1)S(1)}, u32[]{:S(2)}, u32[]{:S(2)}) collective-permute-start(bf16[224,768]{1,0:T(8,128)(2,1)} %own.1), channel_id=1, source_target_pairs={{0,2},{2,0},{1,3},{3,1},{4,6},{6,4},{5,7},{7,5},{8,10},{10,8},{9,1... | collective-permute-start | bytes 1032200 | tf_op jit(solution)/shard_map/ppermute | solution.py:30
  1.5 1.6 %copies.1 = bf16[8,14,1,2,896]{4,3,2,1,0:T(2,128)(2,1)} custom-call(bf16[14,1,2,896]{3,2,1,0:T(2,128)(2,1)} %bitcast.3), custom_call_target="tpu_custom_call" | custom-call | tf_op jit(solution)/shard_map/copies/pallas_call | solution.py:113
  3.1 6.5 %all-to-all-start = ((bf16[8,14,1,2,896]{4,3,2,1,0:T(2,128)(2,1)}), bf16[8,14,1,2,896]{4,3,2,1,0:T(2,128)(2,1)S(1)}, u32[]{:S(2)}, u32[]{:S(2)}) async-start(bf16[8,14,1,2,896]{4,3,2,1,0:T(2,128)(2,1)} %copies.1), calls=%async_computation | async-start | bytes 802816 | tf_op jit(solution)/shard_map/all_to_all | solution.py:26
  9.7 2.9 %collective-permute-start = (bf16[224,768]{1,0:T(8,128)(2,1)}, bf16[224,768]{1,0:T(8,128)(2,1)S(1)}, u32[]{:S(2)}, u32[]{:S(2)}) collective-permute-start(bf16[224,768]{1,0:T(8,128)(2,1)} %own.1), channel_id=1, source_target_pairs={{0,1},{1,0},{2,3},{3,2},{4,5},{5,4},{6,7},{7,6},{8,9},{9,8},{10,11... | collective-permute-start | bytes 1032200 | tf_op jit(solution)/shard_map/ppermute | solution.py:30
  12.5 0.0 collective-permute-done.1.far
  12.6 0.1 collective-permute-start.2
  12.6 1.0 %hot.1 = (bf16[896,768]{1,0:T(8,128)(2,1)S(1)}, bf16[224,896]{1,0:T(8,128)(2,1)S(1)}, bf16[192,768]{1,0:T(8,128)(2,1)S(1)}, f32[192,224]{1,0:T(8,128)S(1)}) custom-call(s32[64]{0:T(128)} %pair_map.1, s32[64]{0:T(128)} %tile_table.1, bf16[224,768]{1,0:T(8,128)(2,1)} %own.1), custom_call_target="tpu_custom_call" | custom-call | flops 374341632 | tf_op jit(solution)/shard_map/hot/pallas_call | solution.py:126
  13.7 0.4 %collective-permute-done.twin = bf16[224,768]{1,0:T(8,128)(2,1)S(1)} collective-permute-done((bf16[224,768]{1,0:T(8,128)(2,1)}, bf16[224,768]{1,0:T(8,128)(2,1)S(1)}, u32[]{:S(2)}, u32[]{:S(2)}) %collective-permute-start) | collective-permute-done | bytes 344096 | tf_op jit(solution)/shard_map/ppermute | solution.py:30
  14.0 0.5 %collective-permute-done.2.fartwin = bf16[224,768]{1,0:T(8,128)(2,1)S(1)} collective-permute-done((bf16[224,768]{1,0:T(8,128)(2,1)S(1)}, bf16[224,768]{1,0:T(8,128)(2,1)S(1)}, u32[]{:S(2)}, u32[]{:S(2)}) %collective-permute-start.2) | collective-permute-done | bytes 344096 | tf_op jit(solution)/shard_map/ppermute | solution.py:30
  14.5 0.9 %pick.1 = (bf16[896,768]{1,0:T(8,128)(2,1)S(1)}, bf16[192,224]{1,0:T(8,128)(2,1)S(1)}) custom-call(bf16[224,768]{1,0:T(8,128)(2,1)S(1)} %collective-permute-done.twin, bf16[224,768]{1,0:T(8,128)(2,1)S(1)} %collective-permute-done.1.far, bf16[224,768]{1,0:T(8,128)(2,1)S(1)} %collective-permute-done.2.fartwin, ...), custom_call_target="tpu_custom_call", output_to_operand_aliasing={{0}: (6, {})} | custom-call | flops 374341632 | tf_op jit(solution)/shard_map/pick/pallas_call | solution.py:145
  15.4 1.1 %all-to-all-done = bf16[8,14,1,2,896]{4,3,2,1,0:T(2,128)(2,1)S(1)} async-done(((bf16[8,14,1,2,896]{4,3,2,1,0:T(2,128)(2,1)}), bf16[8,14,1,2,896]{4,3,2,1,0:T(2,128)(2,1)S(1)}, u32[]{:S(2)}, u32[]{:S(2)}) %all-to-all-start) | async-done | bytes 401440 | tf_op jit(solution)/shard_map/all_to_all | solution.py:26
  16.5 0.2 reshape.9.recv
  16.7 0.8 %mix.1 = bf16[192,768]{1,0:T(8,128)(2,1)S(1)} custom-call(bf16[224,896]{1,0:T(8,128)(2,1)S(1)} %reshape.9.recv, bf16[896,768]{1,0:T(8,128)(2,1)S(1)} %get-tuple-element.15.full, bf16[192,224]{1,0:T(8,128)(2,1)S(1)} %get-tuple-element.16.left), custom_call_target="tpu_custom_call" | custom-call | flops 374341632 | tf_op jit(solution)/shard_map/mix/pallas_call | solution.py:158
  17.5 15.6 %all_to_all.10 = bf16[8,24,768]{2,1,0:T(8,128)(2,1)S(1)} all-to-all(bf16[8,24,768]{2,1,0:T(8,128)(2,1)S(1)} %bitcast.2), channel_id=1, replica_groups={{21,25,29,1,5,9,13,17},{160,32,192,64,224,96,0,128},{23,27,31,3,7,11,15..., dimensions={0} | all-to-all | bytes 589824 | tf_op jit(solution)/shard_map/all_to_all | solution.py:26
  33.1 0.7 %reshape.11 = f32[24,1,768]{2,1,0:T(1,128)} reshape(f32[24,768]{1,0:T(8,128)S(1)} %convert_reduce_fusion) | data formatting | bytes 147456 | tf_op jit(solution)/shard_map/reshape | solution.py:169
  (1 shorter events, 0.0 us)
Async XLA Ops:
  0.0 12.6 %collective-permute-start.1 = (bf16[224,768]{1,0:T(8,128)(2,1)}, bf16[224,768]{1,0:T(8,128)(2,1)S(1)}, u32[]{:S(2)}, u32[]{:S(2)}) collective-permute-start(bf16[224,768]{1,0:T(8,128)(2,1)} %own.1), channel_id=1, source_target_pairs={{0,2},{2,0},{1,3},{3,1},{4,6},{6,4},{5,7},{7,5},{8,10},{10,8},{9,1... | collective-permute-start | bytes 1032200 | tf_op jit(solution)/shard_map/ppermute | solution.py:30
  3.1 13.4 %all-to-all-start = ((bf16[8,14,1,2,896]{4,3,2,1,0:T(2,128)(2,1)}), bf16[8,14,1,2,896]{4,3,2,1,0:T(2,128)(2,1)S(1)}, u32[]{:S(2)}, u32[]{:S(2)}) async-start(bf16[8,14,1,2,896]{4,3,2,1,0:T(2,128)(2,1)} %copies.1), calls=%async_computation | async-start | bytes 802816 | tf_op jit(solution)/shard_map/all_to_all | solution.py:26
  9.7 4.4 %collective-permute-start = (bf16[224,768]{1,0:T(8,128)(2,1)}, bf16[224,768]{1,0:T(8,128)(2,1)S(1)}, u32[]{:S(2)}, u32[]{:S(2)}) collective-permute-start(bf16[224,768]{1,0:T(8,128)(2,1)} %own.1), channel_id=1, source_target_pairs={{0,1},{1,0},{2,3},{3,2},{4,5},{5,4},{6,7},{7,6},{8,9},{9,8},{10,11... | collective-permute-start | bytes 1032200 | tf_op jit(solution)/shard_map/ppermute | solution.py:30
  12.6 2.0 %collective-permute-start.2 = (bf16[224,768]{1,0:T(8,128)(2,1)S(1)}, bf16[224,768]{1,0:T(8,128)(2,1)S(1)}, u32[]{:S(2)}, u32[]{:S(2)}) collective-permute-start(bf16[224,768]{1,0:T(8,128)(2,1)S(1)} %collective-permute-done.1.far), channel_id=1, source_target_pairs={{0,1},{1,0},{2,3},{3,2},{4,5},{5,4},{6,7},{7,6},{8,9},{9,8},{10,11... | collective-permute-start | bytes 1032200 | tf_op jit(solution)/shard_map/ppermute | solution.py:30

commit v5 on v4

--- a/solution.py
+++ b/solution.py
@@ -10,18 +10,20 @@
 
 PAIR = ("z", "xh", "y")
 PLANE_FIRST = 0
-PLANE_ORDER = (5, 6, 7, 0, 1, 2, 3, 4)
-LINE_ORDER = (5, 1, 6, 2, 7, 3, 0, 4)
+FIRST_PLANES = (7, 6, 5, 4, 3, 2, 1, 0)
+NEXT_PLANES = (5, 6, 7, 0, 1, 2, 3, 4)
+FIRST_LINES = (5, 1, 6, 2, 7, 3, 0, 4)
+NEXT_LINES = (5, 1, 6, 2, 7, 3, 0, 4)
 OCC = ("xl", "c")
 SIDE = 8
 
 
-def exchange(x, plane_core):
+def exchange(x, plane_core, plane_order, line_order):
     groups = []
     for fixed in range(SIDE):
         for xl in range(2):
-            plane = [(fixed * SIDE + q) * 4 + xl * 2 + plane_core for q in PLANE_ORDER]
-            line = [(z * SIDE + fixed) * 4 + xl * 2 + 1 - plane_core for z in LINE_ORDER]
+            plane = [(fixed * SIDE + q) * 4 + xl * 2 + plane_core for q in plane_order]
+            line = [(z * SIDE + fixed) * 4 + xl * 2 + 1 - plane_core for z in line_order]
             groups += [plane, line]
     return lax.all_to_all(x, PAIR + OCC, 0, 0, tiled=True, axis_index_groups=groups)
 
@@ -51,7 +53,7 @@
     r = lax.broadcasted_iota(jnp.int32, (k, 128), 0)
     goal = jnp.zeros((k, 128), jnp.int32)
     for s in range(SIDE):
-        source = jnp.where(plane_first, z * SIDE + PLANE_ORDER[s], LINE_ORDER[s] * SIDE + q)
+        source = jnp.where(plane_first, z * SIDE + FIRST_PLANES[s], FIRST_LINES[s] * SIDE + q)
         goal = jnp.where(r >= s * span, (pairs[source] - s) * sblock, goal)
     goal = goal + r // nocc - lax.broadcasted_iota(jnp.int32, (k, 128), 1)
     for c in range(nbf // 128):
@@ -61,7 +63,7 @@
     line = lax.broadcasted_iota(jnp.int32, (cut, 128), 0)
     part = lax.broadcasted_iota(jnp.int32, (cut, k), 1) % nocc
     for s in range(SIDE):
-        tile = tiles[jnp.where(plane_first, LINE_ORDER[s] * SIDE + q, z * SIDE + PLANE_ORDER[s])]
+        tile = tiles[jnp.where(plane_first, NEXT_LINES[s] * SIDE + q, z * SIDE + NEXT_PLANES[s])]
         i = tile // per
         goal = (tile - i * per) * cut + line - lane
         at = pl.ds(s * cut, cut)
@@ -95,7 +97,7 @@
 
 
 def mix_kernel(recv, full, left, part):
-    half = jnp.dot(recv[...], full[...], preferred_element_type=jnp.float32).astype(jnp.bfloat16)
+    half = jnp.dot(recv[...].reshape(-1, full.shape[0]), full[...], preferred_element_type=jnp.float32).astype(jnp.bfloat16)
     part[...] = jnp.dot(left[...], half, preferred_element_type=jnp.float32).astype(jnp.bfloat16)
 
 
@@ -119,7 +121,7 @@
         compiler_params=small,
         name="copies",
     )(pltpu.with_memory_space_constraint(nat, pltpu.HBM))
-    recv = exchange(send, PLANE_FIRST)
+    recv = exchange(send, PLANE_FIRST, FIRST_PLANES, FIRST_LINES)
     twin = swap(coeffs, "c")
     fartwin = swap(far, "c")
     hbm = pl.BlockSpec(memory_space=pltpu.HBM)
@@ -163,8 +165,8 @@
         cost_estimate=work,
         compiler_params=small,
         name="mix",
-    )(recv.reshape(k, nbf), full, left)
-    got = exchange(part.reshape(SIDE, cut, nvirt), 1 - PLANE_FIRST)
+    )(recv.reshape(SIDE, sblock, nocc, nbf), full, left)
+    got = exchange(part.reshape(SIDE, cut, nvirt), 1 - PLANE_FIRST, NEXT_PLANES, NEXT_LINES)
     out = got.astype(jnp.float32).sum(0)
     return out.reshape(cut, 1, nvirt)
 

time: 34.2 us -> 33.5 us (0.980)
  the two profiles are of different devices: /device:TPU:8 before, /device:TPU:4 now
where the time goes in v5:
time: 33.5 us; the launch traced here: 33.2 us
  blocking collectives  15.6 us (47%)
  starting transfers between devices  10.7 us (32%)
  Pallas kernels  4.28 us (13%)
  waiting for transfers between devices  1.88 us (6%)
  local copies, waits for them, and re-layouts  0.68 us (2%)
    all_to_all x1, blocking collectives, exchange(): lax.all_to_all(x, PAIR + OCC, 0, 0, tiled=True, axis_index_groups=groups)  15.6 us
    all_to_all x1, starting transfers between devices, exchange(): lax.all_to_all(x, PAIR + OCC, 0, 0, tiled=True, axis_index_groups=groups)  6.4 us
    ppermute x3, starting transfers between devices, swap(): return lax.ppermute(x, axis, [(0, 1), (1, 0)])  4.32 us
    pallas_call x1, Pallas kernels, layer(): pl.pallas_call(copies_kernel, out_shape=pltpu.HBM((SIDE, *nat.shape), nat...  1.63 us
    all_to_all x1, waiting for transfers between devices, exchange(): lax.all_to_all(x, PAIR + OCC, 0, 0, tiled=True, axis_index_groups=groups)  1.01 us
    pallas_call x1, Pallas kernels, layer(): pl.pallas_call(functools.partial(hot_kernel, sblock, nocc, cut), out_shap...  1 us
    ppermute x3, waiting for transfers between devices, swap(): return lax.ppermute(x, axis, [(0, 1), (1, 0)])  0.88 us
    pallas_call x1, Pallas kernels, layer(): pl.pallas_call(pick_kernel, out_shape=(jax.ShapeDtypeStruct((nbf, nvirt),...  0.87 us
  transfers between devices with their start and end apart: 4, of which 3 were waited for; matrix products, arithmetic and copies ran while one was open for 0% of the time, Pallas kernels for 11%

profile of v5, /device:TPU:4, one launch (start us, length us, event | category | flops | bytes accessed | tf_op | source)
XLA Modules:
  0.0 33.2 jit_solution(17207205222282104933)
XLA Ops:
  0.0 1.2 %collective-permute-start.1 = (bf16[224,768]{1,0:T(8,128)(2,1)}, bf16[224,768]{1,0:T(8,128)(2,1)S(1)}, u32[]{:S(2)}, u32[]{:S(2)}) collective-permute-start(bf16[224,768]{1,0:T(8,128)(2,1)} %own.1), channel_id=1, source_target_pairs={{0,2},{2,0},{1,3},{3,1},{4,6},{6,4},{5,7},{7,5},{8,10},{10,8},{9,1... | collective-permute-start | bytes 1032200 | tf_op jit(solution)/shard_map/ppermute | solution.py:32
  1.2 1.6 %copies.1 = bf16[8,14,1,2,896]{4,3,2,1,0:T(2,128)(2,1)} custom-call(bf16[14,1,2,896]{3,2,1,0:T(2,128)(2,1)} %bitcast.7), custom_call_target="tpu_custom_call" | custom-call | tf_op jit(solution)/shard_map/copies/pallas_call | solution.py:115
  2.8 6.4 %all-to-all-start = ((bf16[8,14,1,2,896]{4,3,1,2,0:T(2,128)(2,1)}), bf16[8,14,1,2,896]{4,3,1,2,0:T(2,128)(2,1)S(1)}, u32[]{:S(2)}, u32[]{:S(2)}) async-start(bf16[8,14,1,2,896]{4,3,1,2,0:T(2,128)(2,1)} %bitcast.6), calls=%async_computation | async-start | bytes 802816 | tf_op jit(solution)/shard_map/all_to_all | solution.py:28
  9.2 3.0 %collective-permute-start = (bf16[224,768]{1,0:T(8,128)(2,1)}, bf16[224,768]{1,0:T(8,128)(2,1)S(1)}, u32[]{:S(2)}, u32[]{:S(2)}) collective-permute-start(bf16[224,768]{1,0:T(8,128)(2,1)} %own.1), channel_id=1, source_target_pairs={{0,1},{1,0},{2,3},{3,2},{4,5},{5,4},{6,7},{7,6},{8,9},{9,8},{10,11... | collective-permute-start | bytes 1032200 | tf_op jit(solution)/shard_map/ppermute | solution.py:32
  12.3 0.0 collective-permute-done.1.far
  12.3 0.1 collective-permute-start.2
  12.4 1.0 %hot.1 = (bf16[896,768]{1,0:T(8,128)(2,1)S(1)}, bf16[224,896]{1,0:T(8,128)(2,1)S(1)}, bf16[192,768]{1,0:T(8,128)(2,1)S(1)}, f32[192,224]{1,0:T(8,128)S(1)}) custom-call(s32[64]{0:T(128)} %pair_map.1, s32[64]{0:T(128)} %tile_table.1, bf16[224,768]{1,0:T(8,128)(2,1)} %own.1), custom_call_target="tpu_custom_call" | custom-call | flops 374341632 | tf_op jit(solution)/shard_map/hot/pallas_call | solution.py:128
  13.4 0.4 %collective-permute-done.twin = bf16[224,768]{1,0:T(8,128)(2,1)S(1)} collective-permute-done((bf16[224,768]{1,0:T(8,128)(2,1)}, bf16[224,768]{1,0:T(8,128)(2,1)S(1)}, u32[]{:S(2)}, u32[]{:S(2)}) %collective-permute-start) | collective-permute-done | bytes 344096 | tf_op jit(solution)/shard_map/ppermute | solution.py:32
  13.7 0.5 %collective-permute-done.2.fartwin = bf16[224,768]{1,0:T(8,128)(2,1)S(1)} collective-permute-done((bf16[224,768]{1,0:T(8,128)(2,1)S(1)}, bf16[224,768]{1,0:T(8,128)(2,1)S(1)}, u32[]{:S(2)}, u32[]{:S(2)}) %collective-permute-start.2) | collective-permute-done | bytes 344096 | tf_op jit(solution)/shard_map/ppermute | solution.py:32
  14.2 0.9 %pick.1 = (bf16[896,768]{1,0:T(8,128)(2,1)S(1)}, bf16[192,224]{1,0:T(8,128)(2,1)S(1)}) custom-call(bf16[224,768]{1,0:T(8,128)(2,1)S(1)} %collective-permute-done.twin, bf16[224,768]{1,0:T(8,128)(2,1)S(1)} %collective-permute-done.1.far, bf16[224,768]{1,0:T(8,128)(2,1)S(1)} %collective-permute-done.2.fartwin, ...), custom_call_target="tpu_custom_call", output_to_operand_aliasing={{0}: (6, {})} | custom-call | flops 374341632 | tf_op jit(solution)/shard_map/pick/pallas_call | solution.py:147
  15.1 1.0 %all-to-all-done = bf16[8,14,1,2,896]{4,3,1,2,0:T(2,128)(2,1)S(1)} async-done(((bf16[8,14,1,2,896]{4,3,1,2,0:T(2,128)(2,1)}), bf16[8,14,1,2,896]{4,3,1,2,0:T(2,128)(2,1)S(1)}, u32[]{:S(2)}, u32[]{:S(2)}) %all-to-all-start) | async-done | bytes 401440 | tf_op jit(solution)/shard_map/all_to_all | solution.py:28
  16.1 0.8 %mix.1 = bf16[192,768]{1,0:T(8,128)(2,1)S(1)} custom-call(bf16[8,14,2,896]{3,2,1,0:T(2,128)(2,1)S(1)} %bitcast.4, bf16[896,768]{1,0:T(8,128)(2,1)S(1)} %get-tuple-element.15.full, bf16[192,224]{1,0:T(8,128)(2,1)S(1)} %get-tuple-element.16.left), custom_call_target="tpu_custom_call" | custom-call | flops 374341632 | tf_op jit(solution)/shard_map/mix/pallas_call | solution.py:160
  16.9 15.6 %all_to_all.10 = bf16[8,24,768]{2,1,0:T(8,128)(2,1)S(1)} all-to-all(bf16[8,24,768]{2,1,0:T(8,128)(2,1)S(1)} %bitcast.5), channel_id=1, replica_groups={{21,25,29,1,5,9,13,17},{160,32,192,64,224,96,0,128},{23,27,31,3,7,11,15..., dimensions={0} | all-to-all | bytes 589824 | tf_op jit(solution)/shard_map/all_to_all | solution.py:28
  32.5 0.7 %reshape.11 = f32[24,1,768]{2,1,0:T(1,128)} reshape(f32[24,768]{1,0:T(8,128)S(1)} %convert_reduce_fusion) | data formatting | bytes 147456 | tf_op jit(solution)/shard_map/reshape | solution.py:171
  (1 shorter events, 0.0 us)
Async XLA Ops:
  0.0 12.3 %collective-permute-start.1 = (bf16[224,768]{1,0:T(8,128)(2,1)}, bf16[224,768]{1,0:T(8,128)(2,1)S(1)}, u32[]{:S(2)}, u32[]{:S(2)}) collective-permute-start(bf16[224,768]{1,0:T(8,128)(2,1)} %own.1), channel_id=1, source_target_pairs={{0,2},{2,0},{1,3},{3,1},{4,6},{6,4},{5,7},{7,5},{8,10},{10,8},{9,1... | collective-permute-start | bytes 1032200 | tf_op jit(solution)/shard_map/ppermute | solution.py:32
  2.8 13.3 %all-to-all-start = ((bf16[8,14,1,2,896]{4,3,1,2,0:T(2,128)(2,1)}), bf16[8,14,1,2,896]{4,3,1,2,0:T(2,128)(2,1)S(1)}, u32[]{:S(2)}, u32[]{:S(2)}) async-start(bf16[8,14,1,2,896]{4,3,1,2,0:T(2,128)(2,1)} %bitcast.6), calls=%async_computation | async-start | bytes 802816 | tf_op jit(solution)/shard_map/all_to_all | solution.py:28
  9.2 4.5 %collective-permute-start = (bf16[224,768]{1,0:T(8,128)(2,1)}, bf16[224,768]{1,0:T(8,128)(2,1)S(1)}, u32[]{:S(2)}, u32[]{:S(2)}) collective-permute-start(bf16[224,768]{1,0:T(8,128)(2,1)} %own.1), channel_id=1, source_target_pairs={{0,1},{1,0},{2,3},{3,2},{4,5},{5,4},{6,7},{7,6},{8,9},{9,8},{10,11... | collective-permute-start | bytes 1032200 | tf_op jit(solution)/shard_map/ppermute | solution.py:32
  12.3 2.0 %collective-permute-start.2 = (bf16[224,768]{1,0:T(8,128)(2,1)S(1)}, bf16[224,768]{1,0:T(8,128)(2,1)S(1)}, u32[]{:S(2)}, u32[]{:S(2)}) collective-permute-start(bf16[224,768]{1,0:T(8,128)(2,1)S(1)} %collective-permute-done.1.far), channel_id=1, source_target_pairs={{0,1},{1,0},{2,3},{3,2},{4,5},{5,4},{6,7},{7,6},{8,9},{9,8},{10,11... | collective-permute-start | bytes 1032200 | tf_op jit(solution)/shard_map/ppermute | solution.py:32

commit v6 on v5

--- a/solution.py
+++ b/solution.py
@@ -9,9 +9,9 @@
 
 
 PAIR = ("z", "xh", "y")
-PLANE_FIRST = 0
-FIRST_PLANES = (7, 6, 5, 4, 3, 2, 1, 0)
-NEXT_PLANES = (5, 6, 7, 0, 1, 2, 3, 4)
+PLANE_FIRST = 1
+FIRST_PLANES = (2, 3, 4, 5, 6, 7, 0, 1)
+NEXT_PLANES = (6, 7, 0, 1, 2, 3, 4, 5)
 FIRST_LINES = (5, 1, 6, 2, 7, 3, 0, 4)
 NEXT_LINES = (5, 1, 6, 2, 7, 3, 0, 4)
 OCC = ("xl", "c")
@@ -85,11 +85,8 @@
     left[...] = (both * mine[...]).astype(jnp.bfloat16)
 
 
-def copies_kernel(rows, out, held, sem, sems):
-    get = pltpu.make_async_copy(rows, held, sem)
-    get.start()
-    get.wait()
-    puts = [pltpu.make_async_copy(held, out.at[k], sems.at[k]) for k in range(SIDE)]
+def copies_kernel(rows, out, sems):
+    puts = [pltpu.make_async_copy(rows, out.at[k], sems.at[k]) for k in range(SIDE)]
     for c in puts:
         c.start()
     for c in puts:
@@ -115,12 +112,14 @@
     send = pl.pallas_call(
         copies_kernel,
         out_shape=pltpu.HBM((SIDE, *nat.shape), nat.dtype),
-        in_specs=[pl.BlockSpec(memory_space=pltpu.HBM)],
+        in_specs=[vmem],
         out_specs=pl.BlockSpec(memory_space=pltpu.HBM),
-        scratch_shapes=[pltpu.VMEM(nat.shape, nat.dtype), pltpu.SemaphoreType.DMA, pltpu.SemaphoreType.DMA((SIDE,))],
+        scratch_shapes=[
+            pltpu.SemaphoreType.DMA((SIDE,)),
+        ],
         compiler_params=small,
         name="copies",
-    )(pltpu.with_memory_space_constraint(nat, pltpu.HBM))
+    )(nat)
     recv = exchange(send, PLANE_FIRST, FIRST_PLANES, FIRST_LINES)
     twin = swap(coeffs, "c")
     fartwin = swap(far, "c")

time: 33.5 us -> 33.6 us (level)
  the two profiles are of different devices: /device:TPU:4 before, /device:TPU:8 now
where the time goes in v6:
time: 33.6 us; the launch traced here: 33 us
  starting transfers between devices  12.1 us (36%)
  blocking collectives  11.7 us (35%)
  waiting for transfers between devices  4.11 us (12%)
  Pallas kernels  3.48 us (10%)
  local copies, waits for them, and re-layouts  1.48 us (4%)
    all_to_all x1, blocking collectives, exchange(): lax.all_to_all(x, PAIR + OCC, 0, 0, tiled=True, axis_index_groups=groups)  11.7 us
    all_to_all x1, starting transfers between devices, exchange(): lax.all_to_all(x, PAIR + OCC, 0, 0, tiled=True, axis_index_groups=groups)  10.1 us
    all_to_all x1, waiting for transfers between devices, exchange(): lax.all_to_all(x, PAIR + OCC, 0, 0, tiled=True, axis_index_groups=groups)  3.28 us
    ppermute x3, starting transfers between devices, swap(): return lax.ppermute(x, axis, [(0, 1), (1, 0)])  2 us
    pallas_call x1, Pallas kernels, layer(): pl.pallas_call(functools.partial(hot_kernel, sblock, nocc, cut), out_shap...  1 us
    pallas_call x1, Pallas kernels, layer(): pl.pallas_call(pick_kernel, out_shape=(jax.ShapeDtypeStruct((nbf, nvirt),...  0.87 us
    ppermute x3, waiting for transfers between devices, swap(): return lax.ppermute(x, axis, [(0, 1), (1, 0)])  0.83 us
    pallas_call x1, Pallas kernels, layer(): pl.pallas_call(copies_kernel, out_shape=pltpu.HBM((SIDE, *nat.shape), nat...  0.83 us
  transfers between devices with their start and end apart: 4, of which 3 were waited for; matrix products, arithmetic and copies ran while one was open for 0% of the time, Pallas kernels for 8%

profile of v6, /device:TPU:8, one launch (start us, length us, event | category | flops | bytes accessed | tf_op | source)
XLA Modules:
  0.0 33.0 jit_solution(7016895393087900534)
XLA Ops:
  0.0 1.5 %collective-permute-start.1 = (bf16[224,768]{1,0:T(8,128)(2,1)}, bf16[224,768]{1,0:T(8,128)(2,1)S(1)}, u32[]{:S(2)}, u32[]{:S(2)}) collective-permute-start(bf16[224,768]{1,0:T(8,128)(2,1)} %own.1), channel_id=1, source_target_pairs={{0,2},{2,0},{1,3},{3,1},{4,6},{6,4},{5,7},{7,5},{8,10},{10,8},{9,1... | collective-permute-start | bytes 1032200 | tf_op jit(solution)/shard_map/ppermute | solution.py:32
  1.5 0.0 copy-start
  1.5 0.8 %copy-done = bf16[2,14,1,896]{3,0,2,1:T(2,128)(2,1)S(1)} copy-done((bf16[2,14,1,896]{3,0,2,1:T(2,128)(2,1)S(1)}, bf16[2,14,1,896]{3,0,2,1:T(2,128)(2,1)}, u32[]{:S(2)}) %copy-start) | copy-done | bytes 50200
  2.3 0.8 %copies.1 = bf16[8,14,1,2,896]{4,3,2,1,0:T(2,128)(2,1)} custom-call(bf16[14,1,2,896]{3,2,1,0:T(2,128)(2,1)S(1)} %bitcast.6), custom_call_target="tpu_custom_call" | custom-call | tf_op jit(solution)/shard_map/copies/pallas_call | solution.py:112
  3.1 10.1 %all-to-all-start = ((bf16[8,14,1,2,896]{4,3,1,2,0:T(2,128)(2,1)}), bf16[8,14,1,2,896]{4,3,1,2,0:T(2,128)(2,1)S(1)}, u32[]{:S(2)}, u32[]{:S(2)}) async-start(bf16[8,14,1,2,896]{4,3,1,2,0:T(2,128)(2,1)} %bitcast.7), calls=%async_computation | async-start | bytes 802816 | tf_op jit(solution)/shard_map/all_to_all | solution.py:28
  13.3 0.0 collective-permute-start
  13.3 0.0 collective-permute-done.1.far
  13.3 0.5 %collective-permute-start.2 = (bf16[224,768]{1,0:T(8,128)(2,1)S(1)}, bf16[224,768]{1,0:T(8,128)(2,1)S(1)}, u32[]{:S(2)}, u32[]{:S(2)}) collective-permute-start(bf16[224,768]{1,0:T(8,128)(2,1)S(1)} %collective-permute-done.1.far), channel_id=1, source_target_pairs={{0,1},{1,0},{2,3},{3,2},{4,5},{5,4},{6,7},{7,6},{8,9},{9,8},{10,11... | collective-permute-start | bytes 1032200 | tf_op jit(solution)/shard_map/ppermute | solution.py:32
  13.8 1.0 %hot.1 = (bf16[896,768]{1,0:T(8,128)(2,1)S(1)}, bf16[224,896]{1,0:T(8,128)(2,1)S(1)}, bf16[192,768]{1,0:T(8,128)(2,1)S(1)}, f32[192,224]{1,0:T(8,128)S(1)}) custom-call(s32[64]{0:T(128)} %pair_map.1, s32[64]{0:T(128)} %tile_table.1, bf16[224,768]{1,0:T(8,128)(2,1)} %own.1), custom_call_target="tpu_custom_call" | custom-call | flops 374341632 | tf_op jit(solution)/shard_map/hot/pallas_call | solution.py:127
  14.8 0.3 %collective-permute-done.twin = bf16[224,768]{1,0:T(8,128)(2,1)S(1)} collective-permute-done((bf16[224,768]{1,0:T(8,128)(2,1)}, bf16[224,768]{1,0:T(8,128)(2,1)S(1)}, u32[]{:S(2)}, u32[]{:S(2)}) %collective-permute-start) | collective-permute-done | bytes 344096 | tf_op jit(solution)/shard_map/ppermute | solution.py:32
  15.1 0.5 %collective-permute-done.2.fartwin = bf16[224,768]{1,0:T(8,128)(2,1)S(1)} collective-permute-done((bf16[224,768]{1,0:T(8,128)(2,1)S(1)}, bf16[224,768]{1,0:T(8,128)(2,1)S(1)}, u32[]{:S(2)}, u32[]{:S(2)}) %collective-permute-start.2) | collective-permute-done | bytes 344096 | tf_op jit(solution)/shard_map/ppermute | solution.py:32
  15.6 0.9 %pick.1 = (bf16[896,768]{1,0:T(8,128)(2,1)S(1)}, bf16[192,224]{1,0:T(8,128)(2,1)S(1)}) custom-call(bf16[224,768]{1,0:T(8,128)(2,1)S(1)} %collective-permute-done.twin, bf16[224,768]{1,0:T(8,128)(2,1)S(1)} %collective-permute-done.1.far, bf16[224,768]{1,0:T(8,128)(2,1)S(1)} %collective-permute-done.2.fartwin, ...), custom_call_target="tpu_custom_call", output_to_operand_aliasing={{0}: (6, {})} | custom-call | flops 374341632 | tf_op jit(solution)/shard_map/pick/pallas_call | solution.py:146
  16.5 3.3 %all-to-all-done = bf16[8,14,1,2,896]{4,3,1,2,0:T(2,128)(2,1)S(1)} async-done(((bf16[8,14,1,2,896]{4,3,1,2,0:T(2,128)(2,1)}), bf16[8,14,1,2,896]{4,3,1,2,0:T(2,128)(2,1)S(1)}, u32[]{:S(2)}, u32[]{:S(2)}) %all-to-all-start) | async-done | bytes 401440 | tf_op jit(solution)/shard_map/all_to_all | solution.py:28
  19.8 0.8 %mix.1 = bf16[192,768]{1,0:T(8,128)(2,1)S(1)} custom-call(bf16[8,14,2,896]{3,2,1,0:T(2,128)(2,1)S(1)} %bitcast.4, bf16[896,768]{1,0:T(8,128)(2,1)S(1)} %get-tuple-element.15.full, bf16[192,224]{1,0:T(8,128)(2,1)S(1)} %get-tuple-element.16.left), custom_call_target="tpu_custom_call" | custom-call | flops 374341632 | tf_op jit(solution)/shard_map/mix/pallas_call | solution.py:159
  20.6 11.7 %all_to_all.10 = bf16[8,24,768]{2,1,0:T(8,128)(2,1)S(1)} all-to-all(bf16[8,24,768]{2,1,0:T(8,128)(2,1)S(1)} %bitcast.5), channel_id=1, replica_groups={{24,28,0,4,8,12,16,20},{161,33,193,65,225,97,1,129},{26,30,2,6,10,14,18..., dimensions={0} | all-to-all | bytes 589824 | tf_op jit(solution)/shard_map/all_to_all | solution.py:28
  32.3 0.7 %reshape.11 = f32[24,1,768]{2,1,0:T(1,128)} reshape(f32[24,768]{1,0:T(8,128)S(1)} %convert_reduce_fusion) | data formatting | bytes 147456 | tf_op jit(solution)/shard_map/reshape | solution.py:170
  (1 shorter events, 0.0 us)
Async XLA Ops:
  0.0 13.3 %collective-permute-start.1 = (bf16[224,768]{1,0:T(8,128)(2,1)}, bf16[224,768]{1,0:T(8,128)(2,1)S(1)}, u32[]{:S(2)}, u32[]{:S(2)}) collective-permute-start(bf16[224,768]{1,0:T(8,128)(2,1)} %own.1), channel_id=1, source_target_pairs={{0,2},{2,0},{1,3},{3,1},{4,6},{6,4},{5,7},{7,5},{8,10},{10,8},{9,1... | collective-permute-start | bytes 1032200 | tf_op jit(solution)/shard_map/ppermute | solution.py:32
  1.5 0.8 %copy-start = (bf16[2,14,1,896]{3,0,2,1:T(2,128)(2,1)S(1)}, bf16[2,14,1,896]{3,0,2,1:T(2,128)(2,1)}, u32[]{:S(2)}) copy-start(bf16[2,14,1,896]{3,0,2,1:T(2,128)(2,1)} %param.4) | copy-start | bytes 150532
  3.1 16.7 %all-to-all-start = ((bf16[8,14,1,2,896]{4,3,1,2,0:T(2,128)(2,1)}), bf16[8,14,1,2,896]{4,3,1,2,0:T(2,128)(2,1)S(1)}, u32[]{:S(2)}, u32[]{:S(2)}) async-start(bf16[8,14,1,2,896]{4,3,1,2,0:T(2,128)(2,1)} %bitcast.7), calls=%async_computation | async-start | bytes 802816 | tf_op jit(solution)/shard_map/all_to_all | solution.py:28
  13.3 1.9 %collective-permute-start = (bf16[224,768]{1,0:T(8,128)(2,1)}, bf16[224,768]{1,0:T(8,128)(2,1)S(1)}, u32[]{:S(2)}, u32[]{:S(2)}) collective-permute-start(bf16[224,768]{1,0:T(8,128)(2,1)} %own.1), channel_id=1, source_target_pairs={{0,1},{1,0},{2,3},{3,2},{4,5},{5,4},{6,7},{7,6},{8,9},{9,8},{10,11... | collective-permute-start | bytes 1032200 | tf_op jit(solution)/shard_map/ppermute | solution.py:32
  13.3 2.3 %collective-permute-start.2 = (bf16[224,768]{1,0:T(8,128)(2,1)S(1)}, bf16[224,768]{1,0:T(8,128)(2,1)S(1)}, u32[]{:S(2)}, u32[]{:S(2)}) collective-permute-start(bf16[224,768]{1,0:T(8,128)(2,1)S(1)} %collective-permute-done.1.far), channel_id=1, source_target_pairs={{0,1},{1,0},{2,3},{3,2},{4,5},{5,4},{6,7},{7,6},{8,9},{9,8},{10,11... | collective-permute-start | bytes 1032200 | tf_op jit(solution)/shard_map/ppermute | solution.py:32
